TPU v7x, 512 devices: a whole 4x4x16 slice. The times are simulated.
512 devices in a mesh: rows: 128 (over z, y_lo, x), cols: 4 (over y_hi, core).
Axes of the slice: x: 4, y: 4 (y_hi: 2, y_lo: 2; y = y_hi * 2 + y_lo), z: 16, core: 2. Of those that a mesh axis runs over, the one named last changes fastest.
Arguments:
- lattice: int32 [4096, 16384], P('rows', 'cols'), may hold values from -1 to 1, as said below
- draws: int32 [2, 4096, 16384], P(None, 'rows', 'cols'), may hold values from -2147483648 to 2147483647, as said below
- thresholds: int32 [5], replicated, may hold values from 32 to 256
Outputs:
- final_lattice: int32 [4096, 16384], P('rows', 'cols')
- row_magnetization: float32 [4096], P('rows')
Inputs may be any that keep to these rules, and one draw needn't show every extreme that they name: `lattice`: every entry is -1 or 1. Each word holds four independent draws of 0 to 255: bits 8k to 8k+7 of draws[p] belong to sweep 4p + k.
All inputs are finite; a program needn't handle non-finite values.
Results may differ from a plain program's by a relative error of at most 0.0003.
Values sent between devices are 32-bit elements; how exact they have to be, the bound alone decides.
No kernel may reach another device: no remote copies, remote signals or barrier semaphores. Data moves between devices by JAX's collectives and lax.ppermute only.
A program may use at most 64 MiB of HBM per device.

v0:
```python
import jax
import jax.numpy as jnp
from jax import lax
from jax.experimental import pallas as pl
from jax.experimental.pallas import tpu as pltpu
from jax.sharding import PartitionSpec as P

SWEEPS = 8
LEVELS = 5
GROUPS = 32
LANES = 128
I32 = jnp.int32


def iotas():
    sub = lax.broadcasted_iota(I32, (8, LANES), 0)
    lane = lax.broadcasted_iota(I32, (8, LANES), 1)
    return sub, lane, (sub + lane) % 2 == 0


def srl(x, n):
    return lax.shift_right_logical(x, jnp.full(x.shape, n, I32))


def up_one(x):
    return pltpu.roll(x, 7, 0)


def split_colours(first, second, even):
    moved = up_one(second)
    return jnp.where(even, first, moved), jnp.where(even, moved, first)


def transpose_bits(words, low_half=False):
    a = list(words)
    masks = {16: 0x0000FFFF, 8: 0x00FF00FF, 4: 0x0F0F0F0F, 2: 0x33333333, 1: 0x55555555}
    for j in (16, 8, 4, 2, 1):
        m = jnp.int32(masks[j])
        for k in range(32):
            if k & j:
                continue
            if low_half and j == 16:
                a[k], a[k + j] = a[k] & m, srl(a[k], 16)
                continue
            t = (srl(a[k], j) ^ a[k + j]) & m
            a[k + j] = a[k + j] ^ t
            a[k] = a[k] ^ (t << j)
    return a


def pack_spins(load):
    word = srl(load(0), 1) & 1
    for g in range(1, GROUPS):
        bit = 1 << g if g < 31 else -(1 << 31)
        word = word | (load(g) & jnp.int32(bit))
    return word


def own_kernel(lattice, draws, planes, words):
    _, _, even = iotas()

    def tile(ref, row, g):
        return ref[pl.ds(row, 8), pl.ds(g * LANES, LANES)]

    for q in range(2):
        first = pack_spins(lambda g: tile(lattice, 16 * q, g))
        second = pack_spins(lambda g: tile(lattice, 16 * q + 8, g))
        words[q, 0], words[q, 1] = split_colours(first, second, even)

    def body(n, carry):
        q, p = n // 2, n % 2
        row = pl.multiple_of(q * 16, 16)
        pairs = []
        for g in range(GROUPS):
            cols = pl.ds(g * LANES, LANES)
            pairs.append(split_colours(draws[p, pl.ds(row, 8), cols], draws[p, pl.ds(row + 8, 8), cols], even))
        for c in range(2):
            for b, plane in enumerate(transpose_bits([pair[c] for pair in pairs])):
                planes[q, c, p, b] = plane
        return carry

    lax.fori_loop(0, 4, body, 0)


def sweep_kernel(thresholds, top, bot, h_top, h_own, h_bot, words, planes, final, means, edge0, edge1, side):
    sub, lane, even = iotas()
    odd = jnp.logical_not(even)

    def tile(ref, row, g):
        return ref[pl.ds(row, 8), pl.ds(g * LANES, LANES)]

    state = [[None] * 5, [None] * 5]
    for q, ref in ((0, top), (3, bot)):
        first = pack_spins(lambda g: tile(ref, 0, g))
        second = pack_spins(lambda g: tile(ref, 8, g))
        state[0][q], state[1][q] = split_colours(first, second, even)
    for q in (1, 2):
        for c in range(2):
            state[c][q] = words[q - 1, c]
    side_rows = ((h_top, 0), (h_own, 0), (h_own, 16), (h_bot, 0))
    state[0][4] = state[1][4] = jnp.zeros((8, LANES), I32)
    for q, (ref, row) in enumerate(side_rows):
        pair = split_colours(ref[pl.ds(row, 8), :], ref[pl.ds(row + 8, 8), :], even)
        for c in range(2):
            state[c][4] = state[c][4] | ((srl(pair[c], 1) & 1) << q)

    for n, ref in enumerate((top, bot)):
        pairs = [split_colours(tile(ref, 16, g), tile(ref, 24, g), even) for g in range(GROUPS)]
        for c in range(2):
            for b, plane in enumerate(transpose_bits([pair[c] for pair in pairs])):
                edge0[n, c, b] = plane
    pairs = [split_colours(tile(bot, 32, g), tile(top, 32, g), even) for g in range(GROUPS)]
    for c in range(2):
        for b, plane in enumerate(transpose_bits([pair[c] for pair in pairs])):
            edge1[c, b] = plane
    slots = [jnp.zeros((8, LANES), I32)] * 32
    first_word = ((h_top, 16), (h_own, 32), (h_own, 48), (h_bot, 16))
    for q, (ref, row) in enumerate(first_word):
        slots[q], slots[4 + q] = split_colours(ref[pl.ds(row, 8), :], ref[pl.ds(row + 8, 8), :], even)
    joined = split_colours(h_bot[pl.ds(32, 8), :], h_top[pl.ds(32, 8), :], even)
    for q in range(4):
        if q in (0, 3):
            slots[8 + q], slots[12 + q] = joined
        else:
            row = 64 + 16 * (q - 1)
            slots[8 + q], slots[12 + q] = split_colours(
                h_own[pl.ds(row, 8), :], h_own[pl.ds(row + 8, 8), :], even
            )
    for b, plane in enumerate(transpose_bits(slots, low_half=True)):
        side[b] = plane

    table = []
    for b in range(8):
        r = [-(((thresholds[4 - k] - 1) >> b) & 1) for k in range(LEVELS)]
        table.append((r[0], r[0] ^ r[1], r[0] ^ r[2], r[0] ^ r[1] ^ r[2] ^ r[3], r[0] ^ r[4]))

    at_left, at_right = lane == 0, lane == LANES - 1
    fix = []
    for c in range(2):
        here, there = (even, odd) if c == 0 else (odd, even)
        fix.append(
            (here & (sub == 0), there & (sub == 7), here & (sub == 7), there & (sub == 6))
        )

    def half_sweep(mine, other, c, draw):
        up_prev, up_self, down_self, down_next = fix[c]
        left = [pltpu.roll(w, 1, 1) for w in other]
        right = [pltpu.roll(w, LANES - 1, 1) for w in other]
        side_left = srl(left[0], 31)
        side_right = right[0] & 1
        for q in range(1, 4):
            side_left = side_left | (srl(left[q], 31) << q)
            side_right = side_right | ((right[q] & 1) << q)
        new = []
        for q in range(5):
            w = other[q]
            if q < 4:
                from_side = srl(left[4], q) & 1
                lft = jnp.where(at_left, (left[q] << 1) | from_side, left[q])
                from_side = (right[4] << (31 - q)) & jnp.int32(-(1 << 31))
                rgt = jnp.where(at_right, srl(right[q], 1) | from_side, right[q])
                before = pltpu.roll(other[max(q - 1, 0)], 2, 0)
                after = pltpu.roll(other[min(q + 1, 3)], 6, 0)
            else:
                lft = jnp.where(at_left, side_left, left[4])
                rgt = jnp.where(at_right, side_right, right[4])
                before = pltpu.roll(w, 2, 0) << 1
                after = srl(pltpu.roll(w, 6, 0), 1)
            up = jnp.where(up_prev, before, jnp.where(up_self, w, pltpu.roll(w, 1, 0)))
            down = jnp.where(down_next, after, jnp.where(down_self, w, pltpu.roll(w, 7, 0)))
            s = mine[q]
            lft, rgt, up, down = lft ^ s, rgt ^ s, up ^ s, down ^ s
            s1, c1 = lft ^ rgt, lft & rgt
            s2, c2 = up ^ down, up & down
            k0 = s1 ^ s2
            k1 = (c1 ^ c2) | (s1 & s2)
            k2 = c1 & c2
            k01 = k0 & k1
            above = None
            for b in range(8):
                x = table[b]
                limit = x[0] ^ (k0 & x[1]) ^ (k1 & x[2]) ^ (k01 & x[3]) ^ (k2 & x[4])
                u = draw(q, b)
                above = u & ~limit if above is None else above ^ ((u ^ limit) & (above ^ u))
            new.append(~(s ^ above))
        return new

    def sweep(p, t, a, b):
        def draw(c):
            def plane(q, bit):
                at = 8 * t + bit
                if q == 4:
                    return srl(side[at], 8 * p + 4 * c)
                if q in (1, 2):
                    return planes[q - 1, c, p, at]
                return edge0[q // 3, c, at] if p == 0 else edge1[c, at]

            return plane

        a = half_sweep(a, b, 0, draw(0))
        b = half_sweep(b, a, 1, draw(1))
        return a, b

    a, b = state
    for p in range(2):
        a, b = lax.fori_loop(0, 4, lambda t, ab: sweep(p, t, *ab), (a, b))

    sums = jnp.zeros((8, LANES), jnp.float32)
    for q in (1, 2):
        first = jnp.where(even, a[q], b[q])
        moved = jnp.where(even, b[q], a[q])
        second = pltpu.roll(moved, 1, 0)
        for n, word in enumerate((first, second)):
            row = 16 * (q - 1) + 8 * n
            minus = jnp.sum(lax.population_count(word).astype(jnp.float32), axis=1, keepdims=True)
            mean = (GROUPS * LANES - 2.0 * minus) * (1.0 / (4 * GROUPS * LANES))
            sums = sums + jnp.where(lane == row + sub, mean, 0.0)
            for g in range(GROUPS):
                spin = ((word << (31 - g)) >> 31) | 1
                final[pl.ds(row, 8), pl.ds(g * LANES, LANES)] = spin
    means[...] = jnp.sum(sums, axis=0, keepdims=True)[:, :32]


def shift(x, axis, by):
    count = lax.axis_size(axis)
    return lax.ppermute(x, axis, [(i, (i + by) % count) for i in range(count)])


def on_device(lattice, draws, thresholds):
    down = jnp.concatenate([lattice[16:], draws[0, 16:], draws[1, 24:]], axis=0)
    up = jnp.concatenate([lattice[:16], draws[0, :16], draws[1, :8]], axis=0)
    top = shift(down, "rows", 1)
    bot = shift(up, "rows", -1)
    stacked = jnp.concatenate([lattice, draws[0], draws[1]], axis=0)
    from_left = shift(stacked[:, -LANES:], "cols", 1)
    from_right = shift(stacked[:, :LANES], "cols", -1)
    lane = lax.broadcasted_iota(I32, (1, LANES), 1)
    side = jnp.where(lane < LANES // 2, from_right, from_left)
    h_top = shift(jnp.concatenate([side[16:32], side[48:64], side[88:]], axis=0), "rows", 1)
    h_bot = shift(jnp.concatenate([side[:16], side[32:48], side[64:72]], axis=0), "rows", -1)

    planes, words = pl.pallas_call(
        own_kernel,
        out_shape=(
            jax.ShapeDtypeStruct((2, 2, 2, 32, 8, LANES), I32),
            jax.ShapeDtypeStruct((2, 2, 8, LANES), I32),
        ),
        cost_estimate=pl.CostEstimate(flops=30_000_000, bytes_accessed=2_700_000, transcendentals=0),
    )(lattice, draws)
    vmem = pl.BlockSpec(memory_space=pltpu.VMEM)
    final, means = pl.pallas_call(
        sweep_kernel,
        out_shape=(
            jax.ShapeDtypeStruct((32, GROUPS * LANES), I32),
            jax.ShapeDtypeStruct((1, 32), jnp.float32),
        ),
        in_specs=[pl.BlockSpec(memory_space=pltpu.SMEM)] + [vmem] * 7,
        scratch_shapes=[
            pltpu.VMEM((2, 2, 32, 8, LANES), I32),
            pltpu.VMEM((2, 32, 8, LANES), I32),
            pltpu.VMEM((32, 8, LANES), I32),
        ],
        cost_estimate=pl.CostEstimate(flops=40_000_000, bytes_accessed=2_700_000, transcendentals=0),
    )(thresholds, top, bot, h_top, side, h_bot, words, planes)
    return final, lax.psum(means, "cols").reshape(32)


def solution(mesh):
    in_specs = (P("rows", "cols"), P(None, "rows", "cols"), P())
    out_specs = (P("rows", "cols"), P("rows"))
    return jax.shard_map(
        on_device, mesh=mesh, in_specs=in_specs, out_specs=out_specs, check_vma=False
    )
```

profile of v0, /device:TPU:1, one launch (start us, length us, event | category | flops | bytes accessed | tf_op | source)
XLA Modules:
  0.0 64.4 jit_solution(13287253540004647118)
XLA Ops:
  0.6 1.0 %slice_bitcast_fusion.4 = (s32[8,4096]{1,0:T(8,128)S(1)}, s32[8,4096]{1,0:T(8,128)S(1)}) fusion(s32[2,32,4096]{2,1,0:T(8,128)} %draws.1), kind=kLoop, calls=%fused_computation.6 | loop fusion | bytes 524288 | tf_op jit(solution)/shard_map/squeeze | solution.py:231
  1.6 0.0 copy-start.1
  1.6 1.1 %slice_bitcast_fusion.2 = (s32[16,4096]{1,0:T(8,128)S(1)}, s32[16,4096]{1,0:T(8,128)S(1)}) fusion(s32[2,32,4096]{2,1,0:T(8,128)} %draws.1), kind=kLoop, calls=%fused_computation.4 | loop fusion | bytes 1048576 | tf_op jit(solution)/shard_map/squeeze | solution.py:231
  2.8 0.1 copy-done.1
  2.9 0.0 copy-start
  2.9 4.1 %collective-permute-start = (s32[40,4096]{1,0:T(8,128)S(1)}, s32[40,4096]{1,0:T(8,128)S(1)}, u32[]{:S(2)}, u32[]{:S(2)}) collective-permute-start(s32[40,4096]{1,0:T(8,128)S(1)} %pad_add_fusion), channel_id=1, source_target_pairs={{0,4},{4,8},{8,12},{12,16},{16,20},{20,24},{24,28},{28,32},{32,36}... | collective-permute-start | bytes 1966088 | tf_op jit(solution)/shard_map/ppermute | solution.py:226
  7.1 13.1 %collective-permute-start.1 = (s32[40,4096]{1,0:T(8,128)S(1)}, s32[40,4096]{1,0:T(8,128)}, u32[]{:S(2)}, u32[]{:S(2)}) collective-permute-start(s32[40,4096]{1,0:T(8,128)S(1)} %pad_add_fusion.1), channel_id=1, source_target_pairs={{0,508},{4,0},{8,4},{12,8},{16,12},{20,16},{24,20},{28,24},{32,28}... | collective-permute-start | bytes 1966088 | tf_op jit(solution)/shard_map/ppermute | solution.py:226
  20.2 0.0 copy-done
  20.2 0.1 slice_bitcast_fusion.1
  20.3 5.4 %collective-permute-start.3 = (s32[96,128]{1,0:T(8,128)S(1)}, s32[96,128]{1,0:T(8,128)S(1)}, u32[]{:S(2)}, u32[]{:S(2)}) collective-permute-start(s32[96,128]{1,0:T(8,128)S(1)} %get-tuple-element.10), channel_id=1, source_target_pairs={{0,1},{1,2},{2,3},{3,0},{4,5},{5,6},{6,7},{7,4},{8,9},{9,10},{10,1... | collective-permute-start | bytes 147464 | tf_op jit(solution)/shard_map/ppermute | solution.py:226
  25.7 1.9 %collective-permute-start.2 = (s32[96,128]{1,0:T(8,128)S(1)}, s32[96,128]{1,0:T(8,128)S(1)}, u32[]{:S(2)}, u32[]{:S(2)}) collective-permute-start(s32[96,128]{1,0:T(8,128)S(1)} %get-tuple-element.11), channel_id=1, source_target_pairs={{0,3},{1,0},{2,1},{3,2},{4,7},{5,4},{6,5},{7,6},{8,11},{9,8},{10,9... | collective-permute-start | bytes 147464 | tf_op jit(solution)/shard_map/ppermute | solution.py:226
  27.6 0.0 collective-permute-done.3
  27.6 5.3 %collective-permute-done.2 = s32[96,128]{1,0:T(8,128)S(1)} collective-permute-done((s32[96,128]{1,0:T(8,128)S(1)}, s32[96,128]{1,0:T(8,128)S(1)}, u32[]{:S(2)}, u32[]{:S(2)}) %collective-permute-start.2) | collective-permute-done | bytes 49184 | tf_op jit(solution)/shard_map/ppermute | solution.py:226
  32.9 0.0 copy-start.3
  32.9 0.6 copy-done.3
  33.5 1.9 %collective-permute-start.4 = (s32[40,128]{1,0:T(8,128)S(1)}, s32[40,128]{1,0:T(8,128)S(1)}, u32[]{:S(2)}, u32[]{:S(2)}) collective-permute-start(s32[40,128]{1,0:T(8,128)S(1)} %pad_add_fusion.5), channel_id=1, source_target_pairs={{0,4},{4,8},{8,12},{12,16},{16,20},{20,24},{24,28},{28,32},{32,36}... | collective-permute-start | bytes 61448 | tf_op jit(solution)/shard_map/ppermute | solution.py:226
  35.4 10.9 %collective-permute-start.5 = (s32[40,128]{1,0:T(8,128)S(1)}, s32[40,128]{1,0:T(8,128)S(1)}, u32[]{:S(2)}, u32[]{:S(2)}) collective-permute-start(s32[40,128]{1,0:T(8,128)S(1)} %pad_add_fusion.6), channel_id=1, source_target_pairs={{0,508},{4,0},{8,4},{12,8},{16,12},{20,16},{24,20},{28,24},{32,28}... | collective-permute-start | bytes 61448 | tf_op jit(solution)/shard_map/ppermute | solution.py:226
  46.4 3.1 %shard_map.50 = (s32[2,2,2,32,8,128]{5,4,3,2,1,0:T(8,128)}, s32[2,2,8,128]{3,2,1,0:T(8,128)}) custom-call(s32[32,4096]{1,0:T(8,128)} %lattice.1, s32[2,32,4096]{2,1,0:T(8,128)} %draws.1), custom_call_target="tpu_custom_call" | custom-call | flops 30000000 | bytes 2700000 | tf_op jit(solution)/shard_map/pallas_call | solution.py:242
  49.5 0.0 collective-permute-done.4.h_top
  49.5 0.0 copy-start.4
  49.5 0.0 collective-permute-done.5.h_bot
  49.5 0.0 copy-start.5
  49.5 0.0 collective-permute-done.top
  49.5 0.0 copy-start.2
  49.5 0.0 collective-permute-done.1.bot
  49.5 0.6 copy-done.4
  50.1 0.0 copy-done.5
  50.1 0.3 copy-done.2
  50.4 5.7 %shard_map.51 = (s32[32,4096]{1,0:T(8,128)}, f32[1,32]{1,0:T(1,128)}) custom-call(s32[5]{0:T(128)} %thresholds.1, s32[40,4096]{1,0:T(8,128)} %copy-done.2, s32[40,4096]{1,0:T(8,128)} %collective-permute-done.1.bot, s32[40,128]{1,0:T(8,128)} %copy-done.4, s32[96,128]{1,0:T(8,128)} %copy-done.3, s32[40,128]{1,0:T(8,128)} %copy-done.5, ...), custom_call_target="tpu_custom_call" | custom-call | flops 40000000 | bytes 2700000 | tf_op jit(solution)/shard_map/pallas_call | solution.py:251
  56.0 0.0 copy-start.6
  56.0 0.7 %copy-done.6 = f32[1,32]{1,0:T(1,128)S(1)} copy-done((f32[1,32]{1,0:T(1,128)S(1)}, f32[1,32]{1,0:T(1,128)}, u32[]{:S(2)}) %copy-start.6) | copy-done | bytes 152
  56.7 7.7 %psum.7 = f32[32]{0:T(128)} all-reduce(f32[32]{0:T(128)S(1)} %bitcast.13), channel_id=1, replica_groups=mesh['rows'=128,'cols'=4] {'cols'}, use_global_device_ids=true, to_apply=%region_0.1 | all-reduce | flops 32 | bytes 256 | tf_op jit(solution)/shard_map/psum | solution.py:265
  (10 shorter events, 0.2 us)
Async XLA Ops:
  1.6 1.2 %copy-start.1 = (s32[32,4096]{1,0:T(8,128)S(1)}, s32[32,4096]{1,0:T(8,128)}, u32[]{:S(2)}) copy-start(s32[32,4096]{1,0:T(8,128)} %lattice.1) | copy-start | bytes 1572868
  2.9 17.3 %copy-start = (s32[2,32,4096]{2,1,0:T(8,128)S(1)}, s32[2,32,4096]{2,1,0:T(8,128)}, u32[]{:S(2)}) copy-start(s32[2,32,4096]{2,1,0:T(8,128)} %draws.1) | copy-start | bytes 3145732
  2.9 46.6 %collective-permute-start = (s32[40,4096]{1,0:T(8,128)S(1)}, s32[40,4096]{1,0:T(8,128)S(1)}, u32[]{:S(2)}, u32[]{:S(2)}) collective-permute-start(s32[40,4096]{1,0:T(8,128)S(1)} %pad_add_fusion), channel_id=1, source_target_pairs={{0,4},{4,8},{8,12},{12,16},{16,20},{20,24},{24,28},{28,32},{32,36}... | collective-permute-start | bytes 1966088 | tf_op jit(solution)/shard_map/ppermute | solution.py:226
  7.1 42.5 %collective-permute-start.1 = (s32[40,4096]{1,0:T(8,128)S(1)}, s32[40,4096]{1,0:T(8,128)}, u32[]{:S(2)}, u32[]{:S(2)}) collective-permute-start(s32[40,4096]{1,0:T(8,128)S(1)} %pad_add_fusion.1), channel_id=1, source_target_pairs={{0,508},{4,0},{8,4},{12,8},{16,12},{20,16},{24,20},{28,24},{32,28}... | collective-permute-start | bytes 1966088 | tf_op jit(solution)/shard_map/ppermute | solution.py:226
  20.3 7.3 %collective-permute-start.3 = (s32[96,128]{1,0:T(8,128)S(1)}, s32[96,128]{1,0:T(8,128)S(1)}, u32[]{:S(2)}, u32[]{:S(2)}) collective-permute-start(s32[96,128]{1,0:T(8,128)S(1)} %get-tuple-element.10), channel_id=1, source_target_pairs={{0,1},{1,2},{2,3},{3,0},{4,5},{5,6},{6,7},{7,4},{8,9},{9,10},{10,1... | collective-permute-start | bytes 147464 | tf_op jit(solution)/shard_map/ppermute | solution.py:226
  25.7 7.2 %collective-permute-start.2 = (s32[96,128]{1,0:T(8,128)S(1)}, s32[96,128]{1,0:T(8,128)S(1)}, u32[]{:S(2)}, u32[]{:S(2)}) collective-permute-start(s32[96,128]{1,0:T(8,128)S(1)} %get-tuple-element.11), channel_id=1, source_target_pairs={{0,3},{1,0},{2,1},{3,2},{4,7},{5,4},{6,5},{7,6},{8,11},{9,8},{10,9... | collective-permute-start | bytes 147464 | tf_op jit(solution)/shard_map/ppermute | solution.py:226
  32.9 0.6 copy-start.3
  33.5 16.0 %collective-permute-start.4 = (s32[40,128]{1,0:T(8,128)S(1)}, s32[40,128]{1,0:T(8,128)S(1)}, u32[]{:S(2)}, u32[]{:S(2)}) collective-permute-start(s32[40,128]{1,0:T(8,128)S(1)} %pad_add_fusion.5), channel_id=1, source_target_pairs={{0,4},{4,8},{8,12},{12,16},{16,20},{20,24},{24,28},{28,32},{32,36}... | collective-permute-start | bytes 61448 | tf_op jit(solution)/shard_map/ppermute | solution.py:226
  35.4 14.0 %collective-permute-start.5 = (s32[40,128]{1,0:T(8,128)S(1)}, s32[40,128]{1,0:T(8,128)S(1)}, u32[]{:S(2)}, u32[]{:S(2)}) collective-permute-start(s32[40,128]{1,0:T(8,128)S(1)} %pad_add_fusion.6), channel_id=1, source_target_pairs={{0,508},{4,0},{8,4},{12,8},{16,12},{20,16},{24,20},{28,24},{32,28}... | collective-permute-start | bytes 61448 | tf_op jit(solution)/shard_map/ppermute | solution.py:226
  49.5 0.6 copy-start.4
  49.5 0.6 copy-start.5
  49.5 0.9 %copy-start.2 = (s32[40,4096]{1,0:T(8,128)}, s32[40,4096]{1,0:T(8,128)S(1)}, u32[]{:S(2)}) copy-start(s32[40,4096]{1,0:T(8,128)S(1)} %collective-permute-done.top) | copy-start | bytes 1966084
  56.0 0.7 %copy-start.6 = (f32[1,32]{1,0:T(1,128)S(1)}, f32[1,32]{1,0:T(1,128)}, u32[]{:S(2)}) copy-start(f32[1,32]{1,0:T(1,128)} %get-tuple-element.9) | copy-start | bytes 388
where the time goes:
time: 64.8 us; the launch traced here: 64.4 us
  starting transfers between devices  37.3 us (58%)
  Pallas kernels  8.75 us (14%)
  blocking collectives  7.7 us (12%)
  waiting for transfers between devices  5.27 us (8%)
  local copies, waits for them, and re-layouts  4.39 us (7%)
  between operations  0.84 us (1%)
    ppermute x6, starting transfers between devices, shift(): return lax.ppermute(x, axis, [(i, (i + by) % count) for i in range(count)])  37.3 us
    psum x1, blocking collectives, on_device(): return (final, lax.psum(means, 'cols').reshape(32))  7.7 us
    pallas_call x1, Pallas kernels, on_device(): pl.pallas_call(sweep_kernel, out_shape=(jax.ShapeDtypeStruct((32, GROUPS...  5.67 us
    ppermute x6, waiting for transfers between devices, shift(): return lax.ppermute(x, axis, [(i, (i + by) % count) for i in range(count)])  5.27 us
    pallas_call x1, Pallas kernels, on_device(): pl.pallas_call(own_kernel, out_shape=(jax.ShapeDtypeStruct((2, 2, 2, 32,...  3.08 us
    unnamed x14, local copies, waits for them, and re-layouts  2.16 us
    squeeze x2, local copies, waits for them, and re-layouts, on_device(): up = jnp.concatenate([lattice[:16], draws[0, :16], draws[1, :8]], axis=0)  2.11 us
  transfers between devices with their start and end apart: 6, of which 1 were waited for; matrix products, arithmetic and copies ran while one was open for 0% of the time, Pallas kernels for 5%

commit v1 on v0

--- a/solution.py
+++ b/solution.py
@@ -56,8 +56,14 @@
     return word
 
 
-def own_kernel(lattice, draws, planes, words):
+def own_kernel(thresholds, lattice, draws, planes, words, table):
     _, _, even = iotas()
+
+    for b in range(8):
+        r = [-(((thresholds[LEVELS - 1 - k] - 1) >> b) & 1) for k in range(LEVELS)]
+        forms = (r[0], r[0] ^ r[1], r[0] ^ r[2], r[0] ^ r[1] ^ r[2] ^ r[3], r[0] ^ r[4])
+        for n, form in enumerate(forms):
+            table[b, n] = jnp.full((8, LANES), form, I32)
 
     def tile(ref, row, g):
         return ref[pl.ds(row, 8), pl.ds(g * LANES, LANES)]
@@ -82,12 +88,20 @@
     lax.fori_loop(0, 4, body, 0)
 
 
-def sweep_kernel(thresholds, top, bot, h_top, h_own, h_bot, words, planes, final, means, edge0, edge1, side):
+def sweep_kernel(
+    top, bot, from_partner, from_other, words, planes, table, final, means, edge0, edge1, side
+):
     sub, lane, even = iotas()
     odd = jnp.logical_not(even)
 
     def tile(ref, row, g):
         return ref[pl.ds(row, 8), pl.ds(g * LANES, LANES)]
+
+    def side_tile(q, n, half):
+        if q in (0, 3):
+            ref = bot if q == 3 or (n == 2 and half == 0) else top
+            return tile(ref, (0, 16, 32)[n] + (8 * half if n < 2 else 0), GROUPS)
+        return join_side(from_partner, from_other, 32 * n + 16 * (q - 1) + 8 * half)
 
     state = [[None] * 5, [None] * 5]
     for q, ref in ((0, top), (3, bot)):
@@ -97,10 +111,9 @@
     for q in (1, 2):
         for c in range(2):
             state[c][q] = words[q - 1, c]
-    side_rows = ((h_top, 0), (h_own, 0), (h_own, 16), (h_bot, 0))
     state[0][4] = state[1][4] = jnp.zeros((8, LANES), I32)
-    for q, (ref, row) in enumerate(side_rows):
-        pair = split_colours(ref[pl.ds(row, 8), :], ref[pl.ds(row + 8, 8), :], even)
+    for q in range(4):
+        pair = split_colours(side_tile(q, 0, 0), side_tile(q, 0, 1), even)
         for c in range(2):
             state[c][4] = state[c][4] | ((srl(pair[c], 1) & 1) << q)
 
@@ -114,25 +127,14 @@
         for b, plane in enumerate(transpose_bits([pair[c] for pair in pairs])):
             edge1[c, b] = plane
     slots = [jnp.zeros((8, LANES), I32)] * 32
-    first_word = ((h_top, 16), (h_own, 32), (h_own, 48), (h_bot, 16))
-    for q, (ref, row) in enumerate(first_word):
-        slots[q], slots[4 + q] = split_colours(ref[pl.ds(row, 8), :], ref[pl.ds(row + 8, 8), :], even)
-    joined = split_colours(h_bot[pl.ds(32, 8), :], h_top[pl.ds(32, 8), :], even)
     for q in range(4):
+        slots[q], slots[4 + q] = split_colours(side_tile(q, 1, 0), side_tile(q, 1, 1), even)
         if q in (0, 3):
-            slots[8 + q], slots[12 + q] = joined
+            slots[8 + q], slots[12 + q] = split_colours(side_tile(3, 2, 0), side_tile(0, 2, 1), even)
         else:
-            row = 64 + 16 * (q - 1)
-            slots[8 + q], slots[12 + q] = split_colours(
-                h_own[pl.ds(row, 8), :], h_own[pl.ds(row + 8, 8), :], even
-            )
+            slots[8 + q], slots[12 + q] = split_colours(side_tile(q, 2, 0), side_tile(q, 2, 1), even)
     for b, plane in enumerate(transpose_bits(slots, low_half=True)):
         side[b] = plane
-
-    table = []
-    for b in range(8):
-        r = [-(((thresholds[4 - k] - 1) >> b) & 1) for k in range(LEVELS)]
-        table.append((r[0], r[0] ^ r[1], r[0] ^ r[2], r[0] ^ r[1] ^ r[2] ^ r[3], r[0] ^ r[4]))
 
     at_left, at_right = lane == 0, lane == LANES - 1
     fix = []
@@ -178,7 +180,7 @@
             k01 = k0 & k1
             above = None
             for b in range(8):
-                x = table[b]
+                x = [table[b, n] for n in range(LEVELS)]
                 limit = x[0] ^ (k0 & x[1]) ^ (k1 & x[2]) ^ (k01 & x[3]) ^ (k2 & x[4])
                 u = draw(q, b)
                 above = u & ~limit if above is None else above ^ ((u ^ limit) & (above ^ u))
@@ -221,47 +223,109 @@
     means[...] = jnp.sum(sums, axis=0, keepdims=True)[:, :32]
 
 
+def side_kernel(lattice, draws, to_partner, to_other, sem):
+    even = lax.axis_index("cols") % 2 == 0
+    last = (GROUPS - 1) * LANES
+    copies = []
+    for target, column in ((to_partner, jnp.where(even, last, 0)), (to_other, jnp.where(even, 0, last))):
+        at = pl.ds(pl.multiple_of(column, LANES), LANES)
+        for n, ref in enumerate((lattice, draws.at[0], draws.at[1])):
+            copies.append(pltpu.make_async_copy(ref.at[:, at], target.at[pl.ds(32 * n, 32), :], sem.at[len(copies)]))
+    for copy in copies:
+        copy.start()
+    for copy in copies:
+        copy.wait()
+
+
+def join_side(from_partner, from_other, at):
+    lane = lax.broadcasted_iota(I32, (8, LANES), 1)
+    low = (lane < LANES // 2) == (lax.axis_index("cols") % 2 == 0)
+    return jnp.where(low, from_partner[pl.ds(at, 8), :], from_other[pl.ds(at, 8), :])
+
+
+def rows_kernel(lattice, draws, from_partner, from_other, down, up):
+    for target, parts in (
+        (down, ((0, 16, 16, 0), (1, 16, 16, 16), (2, 24, 8, 32))),
+        (up, ((0, 0, 16, 0), (1, 0, 16, 16), (2, 0, 8, 32))),
+    ):
+        for n, row, rows, at in parts:
+            ref = lattice if n == 0 else draws.at[n - 1]
+            target[pl.ds(at, rows), pl.ds(0, GROUPS * LANES)] = ref[pl.ds(row, rows), :]
+            for r in range(0, rows, 8):
+                target[pl.ds(at + r, 8), pl.ds(GROUPS * LANES, LANES)] = join_side(
+                    from_partner, from_other, 32 * n + row + r
+                )
+
+
 def shift(x, axis, by):
     count = lax.axis_size(axis)
     return lax.ppermute(x, axis, [(i, (i + by) % count) for i in range(count)])
 
 
+def swap(x, axis, first):
+    count = lax.axis_size(axis)
+    pairs = [(i, (i + 1) % count) for i in range(first, count, 2)]
+    return lax.ppermute(x, axis, pairs + [(j, i) for i, j in pairs])
+
+
+def compiler_params():
+    return pltpu.CompilerParams(vmem_limit_bytes=16 << 20)
+
+
 def on_device(lattice, draws, thresholds):
-    down = jnp.concatenate([lattice[16:], draws[0, 16:], draws[1, 24:]], axis=0)
-    up = jnp.concatenate([lattice[:16], draws[0, :16], draws[1, :8]], axis=0)
+    width = GROUPS * LANES
+    vmem, smem = pl.BlockSpec(memory_space=pltpu.VMEM), pl.BlockSpec(memory_space=pltpu.SMEM)
+    hbm = pl.BlockSpec(memory_space=pltpu.HBM)
+    side = jax.ShapeDtypeStruct((96, LANES), I32)
+    to_partner, to_other = pl.pallas_call(
+        side_kernel,
+        out_shape=(side, side),
+        in_specs=[hbm] * 2,
+        out_specs=(vmem,) * 2,
+        scratch_shapes=[pltpu.SemaphoreType.DMA((6,))],
+        compiler_params=compiler_params(),
+        cost_estimate=pl.CostEstimate(flops=100_000, bytes_accessed=200_000, transcendentals=0),
+    )(pltpu.with_memory_space_constraint(lattice, pltpu.HBM), pltpu.with_memory_space_constraint(draws, pltpu.HBM))
+    from_other = swap(to_other, "cols", 1)
+    from_partner = swap(to_partner, "cols", 0)
+
+    rows = jax.ShapeDtypeStruct((40, width + LANES), I32)
+    down, up = pl.pallas_call(
+        rows_kernel,
+        out_shape=(rows, rows),
+        compiler_params=compiler_params(),
+        cost_estimate=pl.CostEstimate(flops=1_000_000, bytes_accessed=3_000_000, transcendentals=0),
+    )(lattice, draws, from_partner, from_other)
     top = shift(down, "rows", 1)
     bot = shift(up, "rows", -1)
-    stacked = jnp.concatenate([lattice, draws[0], draws[1]], axis=0)
-    from_left = shift(stacked[:, -LANES:], "cols", 1)
-    from_right = shift(stacked[:, :LANES], "cols", -1)
-    lane = lax.broadcasted_iota(I32, (1, LANES), 1)
-    side = jnp.where(lane < LANES // 2, from_right, from_left)
-    h_top = shift(jnp.concatenate([side[16:32], side[48:64], side[88:]], axis=0), "rows", 1)
-    h_bot = shift(jnp.concatenate([side[:16], side[32:48], side[64:72]], axis=0), "rows", -1)
-
-    planes, words = pl.pallas_call(
+
+    planes, words, table = pl.pallas_call(
         own_kernel,
         out_shape=(
             jax.ShapeDtypeStruct((2, 2, 2, 32, 8, LANES), I32),
             jax.ShapeDtypeStruct((2, 2, 8, LANES), I32),
+            jax.ShapeDtypeStruct((8, LEVELS, 8, LANES), I32),
         ),
+        in_specs=[smem, vmem, vmem],
+        compiler_params=compiler_params(),
         cost_estimate=pl.CostEstimate(flops=30_000_000, bytes_accessed=2_700_000, transcendentals=0),
-    )(lattice, draws)
-    vmem = pl.BlockSpec(memory_space=pltpu.VMEM)
+    )(thresholds, lattice, draws)
+
     final, means = pl.pallas_call(
         sweep_kernel,
         out_shape=(
-            jax.ShapeDtypeStruct((32, GROUPS * LANES), I32),
+            jax.ShapeDtypeStruct((32, width), I32),
             jax.ShapeDtypeStruct((1, 32), jnp.float32),
         ),
-        in_specs=[pl.BlockSpec(memory_space=pltpu.SMEM)] + [vmem] * 7,
+        in_specs=[vmem] * 7,
         scratch_shapes=[
             pltpu.VMEM((2, 2, 32, 8, LANES), I32),
             pltpu.VMEM((2, 32, 8, LANES), I32),
             pltpu.VMEM((32, 8, LANES), I32),
         ],
+        compiler_params=compiler_params(),
         cost_estimate=pl.CostEstimate(flops=40_000_000, bytes_accessed=2_700_000, transcendentals=0),
-    )(thresholds, top, bot, h_top, side, h_bot, words, planes)
+    )(top, bot, from_partner, from_other, words, planes, table)
     return final, lax.psum(means, "cols").reshape(32)
 
 

time: 64.8 us -> 54.9 us (0.85)
  starting transfers between devices: 37.3 us -> 21.6 us
  waiting for transfers between devices: 5.27 us -> 18.2 us
  local copies, waits for them, and re-layouts: 4.39 us -> 0.01 us
  Pallas kernels: 8.75 us -> 6.34 us
    ppermute x6 -> x2, starting transfers between devices: 37.3 us -> 10.9 us  [shift(): return lax.ppermute(x, axis, [(i, (i + by) % count) for i in range(count)])]
    ppermute x0 -> x2, starting transfers between devices: none -> 10.7 us  [swap(): return lax.ppermute(x, axis, pairs + [(j, i) for i, j in pairs])]
    ppermute x6 -> x2, waiting for transfers between devices: 5.27 us -> 13.2 us  [shift(): return lax.ppermute(x, axis, [(i, (i + by) % count) for i in range(count)])]
    ppermute x0 -> x2, waiting for transfers between devices: none -> 4.98 us  [swap(): return lax.ppermute(x, axis, pairs + [(j, i) for i, j in pairs])]
    squeeze x3 -> x0, local copies, waits for them, and re-layouts: 2.18 us -> none  [the longest x2 2.11 us: on_device(): up = jnp.concatenate([lattice[:16], draws[0, :16], draws[1, :8]], axis=0)]
    unnamed x14 -> x6, local copies, waits for them, and re-layouts: 2.16 us -> 0.01 us
    pallas_call x1, Pallas kernels: 3.08 us -> 1.28 us  [on_device(): pl.pallas_call(own_kernel, out_shape=(jax.ShapeDtypeStruct((2, 2, 2, 32,...]
    pallas_call x1 -> x3, Pallas kernels: 5.67 us -> 5.07 us  [the longest x1 4 us: on_device(): pl.pallas_call(sweep_kernel, out_shape=(jax.ShapeDtypeStruct((32, width),...]
  transfers between devices with their start and end apart: 6 -> 4, of which waited for: 1 -> 3; matrix products, arithmetic and copies ran while one was open for 0% -> 0% of each run, Pallas kernels for 5% -> 2%
where the time goes in v1:
time: 54.9 us; the launch traced here: 54.7 us
  starting transfers between devices  21.6 us (39%)
  waiting for transfers between devices  18.2 us (33%)
  blocking collectives  7.87 us (14%)
  Pallas kernels  6.34 us (12%)
  between operations  0.72 us (1%)
    ppermute x2, waiting for transfers between devices, shift(): return lax.ppermute(x, axis, [(i, (i + by) % count) for i in range(count)])  13.2 us
    ppermute x2, starting transfers between devices, shift(): return lax.ppermute(x, axis, [(i, (i + by) % count) for i in range(count)])  10.9 us
    ppermute x2, starting transfers between devices, swap(): return lax.ppermute(x, axis, pairs + [(j, i) for i, j in pairs])  10.7 us
    psum x1, blocking collectives, on_device(): return (final, lax.psum(means, 'cols').reshape(32))  7.87 us
    ppermute x2, waiting for transfers between devices, swap(): return lax.ppermute(x, axis, pairs + [(j, i) for i, j in pairs])  4.98 us
    pallas_call x1, Pallas kernels, on_device(): pl.pallas_call(sweep_kernel, out_shape=(jax.ShapeDtypeStruct((32, width),...  4 us
    pallas_call x1, Pallas kernels, on_device(): pl.pallas_call(own_kernel, out_shape=(jax.ShapeDtypeStruct((2, 2, 2, 32,...  1.28 us
  transfers between devices with their start and end apart: 4, of which 3 were waited for; matrix products, arithmetic and copies ran while one was open for 0% of the time, Pallas kernels for 2%

profile of v1, /device:TPU:1, one launch (start us, length us, event | category | flops | bytes accessed | tf_op | source)
XLA Modules:
  0.0 54.7 jit_solution(4996309069094964515)
XLA Ops:
  0.6 0.0 copy-start.1
  0.6 0.0 copy-start
  0.6 1.0 %shard_map.50 = (s32[96,128]{1,0:T(8,128)S(1)}, s32[96,128]{1,0:T(8,128)S(1)}) custom-call(s32[32,4096]{1,0:T(8,128)} %lattice.5, s32[2,32,4096]{2,1,0:T(8,128)} %draws.5), custom_call_target="tpu_custom_call" | custom-call | flops 100000 | bytes 200000 | tf_op jit(solution)/shard_map/pallas_call | solution.py:280
  1.6 8.7 %collective-permute-start = (s32[96,128]{1,0:T(8,128)S(1)}, s32[96,128]{1,0:T(8,128)S(1)}, u32[]{:S(2)}, u32[]{:S(2)}) collective-permute-start(s32[96,128]{1,0:T(8,128)S(1)} %get-tuple-element.11), channel_id=1, source_target_pairs={{0,1},{2,3},{1,0},{3,2},{4,5},{6,7},{5,4},{7,6},{8,9},{10,11},{9,8... | collective-permute-start | bytes 147464 | tf_op jit(solution)/shard_map/ppermute | solution.py:268
  10.4 1.9 %collective-permute-start.1 = (s32[96,128]{1,0:T(8,128)S(1)}, s32[96,128]{1,0:T(8,128)S(1)}, u32[]{:S(2)}, u32[]{:S(2)}) collective-permute-start(s32[96,128]{1,0:T(8,128)S(1)} %get-tuple-element.12), channel_id=1, source_target_pairs={{1,2},{3,0},{2,1},{0,3},{5,6},{7,4},{6,5},{4,7},{9,10},{11,8},{10,... | collective-permute-start | bytes 147464 | tf_op jit(solution)/shard_map/ppermute | solution.py:268
  12.3 0.0 collective-permute-done.from_partner
  12.3 5.0 %collective-permute-done.1.from_other = s32[96,128]{1,0:T(8,128)S(1)} collective-permute-done((s32[96,128]{1,0:T(8,128)S(1)}, s32[96,128]{1,0:T(8,128)S(1)}, u32[]{:S(2)}, u32[]{:S(2)}) %collective-permute-start.1) | collective-permute-done | bytes 49184 | tf_op jit(solution)/shard_map/ppermute | solution.py:268
  17.3 0.0 copy-done.1
  17.3 0.0 copy-done
  17.3 0.1 shard_map.51
  17.4 0.0 copy-start.2
  17.4 1.9 %collective-permute-start.2 = (s32[40,4224]{1,0:T(8,128)S(1)}, s32[40,4224]{1,0:T(8,128)S(1)}, u32[]{:S(2)}, u32[]{:S(2)}) collective-permute-start(s32[40,4224]{1,0:T(8,128)S(1)} %get-tuple-element.13), channel_id=1, source_target_pairs={{0,4},{4,8},{8,12},{12,16},{16,20},{20,24},{24,28},{28,32},{32,36}... | collective-permute-start | bytes 2027528 | tf_op jit(solution)/shard_map/ppermute | solution.py:262
  19.3 9.0 %collective-permute-start.3 = (s32[40,4224]{1,0:T(8,128)S(1)}, s32[40,4224]{1,0:T(8,128)S(1)}, u32[]{:S(2)}, u32[]{:S(2)}) collective-permute-start(s32[40,4224]{1,0:T(8,128)S(1)} %get-tuple-element.14), channel_id=1, source_target_pairs={{0,508},{4,0},{8,4},{12,8},{16,12},{20,16},{24,20},{28,24},{32,28}... | collective-permute-start | bytes 2027528 | tf_op jit(solution)/shard_map/ppermute | solution.py:262
  28.3 0.0 copy-done.2
  28.3 1.3 %shard_map.52 = (s32[2,2,2,32,8,128]{5,4,3,2,1,0:T(8,128)S(1)}, s32[2,2,8,128]{3,2,1,0:T(8,128)S(1)}, s32[8,5,8,128]{3,2,1,0:T(8,128)S(1)}) custom-call(s32[5]{0:T(128)S(1)} %copy-done.2, s32[32,4096]{1,0:T(8,128)S(1)} %copy-done.1, s32[2,32,4096]{2,1,0:T(8,128)S(1)} %copy-done), custom_call_target="tpu_custom_call" | custom-call | flops 30000000 | bytes 2700000 | tf_op jit(solution)/shard_map/pallas_call | solution.py:302
  29.6 12.3 %collective-permute-done.2.top = s32[40,4224]{1,0:T(8,128)S(1)} collective-permute-done((s32[40,4224]{1,0:T(8,128)S(1)}, s32[40,4224]{1,0:T(8,128)S(1)}, u32[]{:S(2)}, u32[]{:S(2)}) %collective-permute-start.2) | collective-permute-done | bytes 675872 | tf_op jit(solution)/shard_map/ppermute | solution.py:262
  41.9 0.9 %collective-permute-done.3.bot = s32[40,4224]{1,0:T(8,128)S(1)} collective-permute-done((s32[40,4224]{1,0:T(8,128)S(1)}, s32[40,4224]{1,0:T(8,128)S(1)}, u32[]{:S(2)}, u32[]{:S(2)}) %collective-permute-start.3) | collective-permute-done | bytes 675872 | tf_op jit(solution)/shard_map/ppermute | solution.py:262
  42.8 4.0 %shard_map.53 = (s32[32,4096]{1,0:T(8,128)}, f32[1,32]{1,0:T(1,128)S(1)}) custom-call(s32[40,4224]{1,0:T(8,128)S(1)} %collective-permute-done.2.top, s32[40,4224]{1,0:T(8,128)S(1)} %collective-permute-done.3.bot, s32[96,128]{1,0:T(8,128)S(1)} %collective-permute-done.from_partner, s32[96,128]{1,0:T(8,128)S(1)} %collective-permute-done.1.from_other, ...), custom_call_target="tpu_custom_call" | custom-call | flops 40000000 | bytes 2700000 | tf_op jit(solution)/shard_map/pallas_call | solution.py:314
  46.8 7.9 %psum.7 = f32[32]{0:T(128)} all-reduce(f32[32]{0:T(128)S(1)} %bitcast.1), channel_id=1, replica_groups=mesh['rows'=128,'cols'=4] {'cols'}, use_global_device_ids=true, to_apply=%region_0.0 | all-reduce | flops 32 | bytes 256 | tf_op jit(solution)/shard_map/psum | solution.py:329
Async XLA Ops:
  0.6 16.7 %copy-start.1 = (s32[32,4096]{1,0:T(8,128)S(1)}, s32[32,4096]{1,0:T(8,128)}, u32[]{:S(2)}) copy-start(s32[32,4096]{1,0:T(8,128)} %lattice.5) | copy-start | bytes 1572868
  0.6 16.7 %copy-start = (s32[2,32,4096]{2,1,0:T(8,128)S(1)}, s32[2,32,4096]{2,1,0:T(8,128)}, u32[]{:S(2)}) copy-start(s32[2,32,4096]{2,1,0:T(8,128)} %draws.5) | copy-start | bytes 3145732
  1.6 10.7 %collective-permute-start = (s32[96,128]{1,0:T(8,128)S(1)}, s32[96,128]{1,0:T(8,128)S(1)}, u32[]{:S(2)}, u32[]{:S(2)}) collective-permute-start(s32[96,128]{1,0:T(8,128)S(1)} %get-tuple-element.11), channel_id=1, source_target_pairs={{0,1},{2,3},{1,0},{3,2},{4,5},{6,7},{5,4},{7,6},{8,9},{10,11},{9,8... | collective-permute-start | bytes 147464 | tf_op jit(solution)/shard_map/ppermute | solution.py:268
  10.4 6.9 %collective-permute-start.1 = (s32[96,128]{1,0:T(8,128)S(1)}, s32[96,128]{1,0:T(8,128)S(1)}, u32[]{:S(2)}, u32[]{:S(2)}) collective-permute-start(s32[96,128]{1,0:T(8,128)S(1)} %get-tuple-element.12), channel_id=1, source_target_pairs={{1,2},{3,0},{2,1},{0,3},{5,6},{7,4},{6,5},{4,7},{9,10},{11,8},{10,... | collective-permute-start | bytes 147464 | tf_op jit(solution)/shard_map/ppermute | solution.py:268
  17.4 10.9 %copy-start.2 = (s32[5]{0:T(128)S(1)}, s32[5]{0:T(128)}, u32[]{:S(2)}) copy-start(s32[5]{0:T(128)} %thresholds.1) | copy-start | bytes 64
  17.4 24.5 %collective-permute-start.2 = (s32[40,4224]{1,0:T(8,128)S(1)}, s32[40,4224]{1,0:T(8,128)S(1)}, u32[]{:S(2)}, u32[]{:S(2)}) collective-permute-start(s32[40,4224]{1,0:T(8,128)S(1)} %get-tuple-element.13), channel_id=1, source_target_pairs={{0,4},{4,8},{8,12},{12,16},{16,20},{20,24},{24,28},{28,32},{32,36}... | collective-permute-start | bytes 2027528 | tf_op jit(solution)/shard_map/ppermute | solution.py:262
  19.3 23.5 %collective-permute-start.3 = (s32[40,4224]{1,0:T(8,128)S(1)}, s32[40,4224]{1,0:T(8,128)S(1)}, u32[]{:S(2)}, u32[]{:S(2)}) collective-permute-start(s32[40,4224]{1,0:T(8,128)S(1)} %get-tuple-element.14), channel_id=1, source_target_pairs={{0,508},{4,0},{8,4},{12,8},{16,12},{20,16},{24,20},{28,24},{32,28}... | collective-permute-start | bytes 2027528 | tf_op jit(solution)/shard_map/ppermute | solution.py:262

commit v2 on v1

v2 whole, which is shorter than its diff:
```python
import jax
import jax.numpy as jnp
from jax import lax
from jax.experimental import pallas as pl
from jax.experimental.pallas import tpu as pltpu
from jax.sharding import PartitionSpec as P


SWEEPS = 8
LEVELS = 5
GROUPS = 32
LANES = 128
I32 = jnp.int32


def iotas():
    sub = lax.broadcasted_iota(I32, (8, LANES), 0)
    lane = lax.broadcasted_iota(I32, (8, LANES), 1)
    return sub, lane, (sub + lane) % 2 == 0


def srl(x, n):
    return lax.shift_right_logical(x, jnp.full(x.shape, n, I32))


def up_one(x):
    return pltpu.roll(x, 7, 0)


def split_colours(first, second, even):
    moved = up_one(second)
    return jnp.where(even, first, moved), jnp.where(even, moved, first)


def transpose_bits(words, low_half=False):
    a = list(words)
    masks = {16: 0x0000FFFF, 8: 0x00FF00FF, 4: 0x0F0F0F0F, 2: 0x33333333, 1: 0x55555555}
    for j in (16, 8, 4, 2, 1):
        m = jnp.int32(masks[j])
        for k in range(32):
            if k & j:
                continue
            if low_half and j == 16:
                a[k], a[k + j] = a[k] & m, srl(a[k], 16)
                continue
            t = (srl(a[k], j) ^ a[k + j]) & m
            a[k + j] = a[k + j] ^ t
            a[k] = a[k] ^ (t << j)
    return a


def pack_spins(load):
    word = srl(load(0), 1) & 1
    for g in range(1, GROUPS):
        bit = 1 << g if g < 31 else -(1 << 31)
        word = word | (load(g) & jnp.int32(bit))
    return word


def own_kernel(thresholds, lattice, draws, accept, words, table, planes, clears):
    _, _, even = iotas()

    bits = [[-(((thresholds[LEVELS - 1 - k] - 1) >> b) & 1) for b in range(8)] for k in range(LEVELS)]
    for b in range(8):
        r = [bits[k][b] for k in range(LEVELS)]
        forms = (r[0], r[0] ^ r[1], r[0] ^ r[2], r[0] ^ r[1] ^ r[2] ^ r[3], r[0] ^ r[4])
        for n, form in enumerate(forms):
            table[b, n] = jnp.full((8, LANES), form, I32)
        for k in range(LEVELS):
            clears[b, k] = jnp.full((8, LANES), ~bits[k][b], I32)

    def tile(ref, row, g):
        return ref[pl.ds(row, 8), pl.ds(g * LANES, LANES)]

    for q in range(2):
        first = pack_spins(lambda g: tile(lattice, 16 * q, g))
        second = pack_spins(lambda g: tile(lattice, 16 * q + 8, g))
        words[q, 0], words[q, 1] = split_colours(first, second, even)

    def body(n, carry):
        q, c, p = n // 4, n // 2 % 2, n % 2
        row = pl.multiple_of(q * 16, 16)
        mine = even == (c == 0)
        inputs = []
        for g in range(GROUPS):
            cols = pl.ds(g * LANES, LANES)
            inputs.append(jnp.where(mine, draws[p, pl.ds(row, 8), cols], up_one(draws[p, pl.ds(row + 8, 8), cols])))
        for b, plane in enumerate(transpose_bits(inputs)):
            planes[b] = plane

        def one_sweep(t, carry):
            u = [planes[8 * t + b] for b in range(8)]
            below = []
            for k in range(LEVELS):
                clear = [clears[b, k] for b in range(8)]
                z = clear[0]
                for b in range(8):
                    z = z & (u[b] ^ clear[b])
                    z = ~(z ^ clear[b]) if b == 7 else z ^ (clear[b] ^ clear[b + 1])
                below.append(z)
            r = below
            at = 4 * p + t
            accept[q, c, at, 0] = r[0]
            accept[q, c, at, 1] = r[0] ^ r[1]
            accept[q, c, at, 2] = r[0] ^ r[2]
            accept[q, c, at, 3] = r[0] ^ r[1] ^ r[2] ^ r[3]
            accept[q, c, at, 4] = r[0] ^ r[4]
            return carry

        return lax.fori_loop(0, 4, one_sweep, carry)

    lax.fori_loop(0, 8, body, 0)


def sweep_kernel(
    near, far, side, words, accept, table, final, means, edge0, edge1, side_planes, spins, sems
):
    sub, lane, even = iotas()
    odd = jnp.logical_not(even)

    def tile(ref, row, g):
        return ref[pl.ds(row, 8), pl.ds(g * LANES, LANES)]

    rows_even = rows_are_even()

    def edge_tile(q, row, g):
        at_near, at_far = tile(near, row, g), tile(far, row, g)
        return jnp.where(rows_even, at_far, at_near) if q == 0 else jnp.where(rows_even, at_near, at_far)

    def side_tile(q, n, half):
        if q in (0, 3):
            return edge_tile(q, (0, 16, 32)[n] + (8 * half if n < 2 else 0), GROUPS)
        return side[pl.ds(32 * n + 16 * (q - 1) + 8 * half, 8), :]

    state = [[None] * 5, [None] * 5]
    edges = []
    for ref in (near, far):
        first = pack_spins(lambda g: tile(ref, 0, g))
        second = pack_spins(lambda g: tile(ref, 8, g))
        edges.append(split_colours(first, second, even))
    for c in range(2):
        state[c][0] = jnp.where(rows_even, edges[1][c], edges[0][c])
        state[c][3] = jnp.where(rows_even, edges[0][c], edges[1][c])
    for q in (1, 2):
        for c in range(2):
            state[c][q] = words[q - 1, c]
    state[0][4] = state[1][4] = jnp.zeros((8, LANES), I32)
    for q in range(4):
        pair = split_colours(side_tile(q, 0, 0), side_tile(q, 0, 1), even)
        for c in range(2):
            state[c][4] = state[c][4] | ((srl(pair[c], 1) & 1) << q)

    for n, ref in enumerate((near, far)):
        pairs = [split_colours(tile(ref, 16, g), tile(ref, 24, g), even) for g in range(GROUPS)]
        for c in range(2):
            for b, plane in enumerate(transpose_bits([pair[c] for pair in pairs])):
                edge0[n, c, b] = plane
    pairs = [split_colours(edge_tile(3, 32, g), edge_tile(0, 32, g), even) for g in range(GROUPS)]
    for c in range(2):
        for b, plane in enumerate(transpose_bits([pair[c] for pair in pairs])):
            edge1[c, b] = plane
    slots = [jnp.zeros((8, LANES), I32)] * 32
    for q in range(4):
        slots[q], slots[4 + q] = split_colours(side_tile(q, 1, 0), side_tile(q, 1, 1), even)
        if q in (0, 3):
            slots[8 + q], slots[12 + q] = split_colours(side_tile(3, 2, 0), side_tile(0, 2, 1), even)
        else:
            slots[8 + q], slots[12 + q] = split_colours(side_tile(q, 2, 0), side_tile(q, 2, 1), even)
    for b, plane in enumerate(transpose_bits(slots, low_half=True)):
        side_planes[b] = plane

    at_left, at_right = lane == 0, lane == LANES - 1
    fix = []
    for c in range(2):
        here, there = (even, odd) if c == 0 else (odd, even)
        fix.append((here & (sub == 0), there & (sub == 7), here & (sub == 7), there & (sub == 6)))

    edge_at = {0: jnp.where(rows_even, 1, 0), 3: jnp.where(rows_even, 0, 1)}

    def half_sweep(mine, other, c, t):
        p, at = t // 4, t % 4
        joined = p == 1
        blocks = (0, 1, 2, 4) if joined else (0, 1, 2, 3, 4)
        up_prev, up_self, down_self, down_next = fix[c]
        left = {q: pltpu.roll(other[q], 1, 1) for q in blocks}
        right = {q: pltpu.roll(other[q], LANES - 1, 1) for q in blocks}
        side_left = jnp.zeros((8, LANES), I32)
        side_right = jnp.zeros((8, LANES), I32)
        for q in blocks[:-1]:
            if joined and q == 0:
                side_left = side_left | (srl(left[0], 31) * 9)
                side_right = side_right | ((right[0] & 1) * 9)
            else:
                side_left = side_left | (srl(left[q], 31) << q)
                side_right = side_right | ((right[q] & 1) << q)
        mine_first = even if c == 0 else odd
        new = {}
        for q in blocks:
            w, s = other[q], mine[q]
            if q < 4:
                if joined and q == 0:
                    from_left = jnp.where(mine_first, srl(left[4], 3), left[4]) & 1
                    from_right = jnp.where(mine_first, right[4] << 28, right[4] << 31) & jnp.int32(-(1 << 31))
                    before, after = other[2], other[1]
                else:
                    from_left = srl(left[4], q) & 1
                    from_right = (right[4] << (31 - q)) & jnp.int32(-(1 << 31))
                    before = other[max(q - 1, 0)]
                    after = other[0 if joined and q == 2 else min(q + 1, 3)]
                lft = jnp.where(at_left, (left[q] << 1) | from_left, left[q])
                rgt = jnp.where(at_right, srl(right[q], 1) | from_right, right[q])
                before, after = pltpu.roll(before, 2, 0), pltpu.roll(after, 6, 0)
            else:
                lft = jnp.where(at_left, side_left, left[4])
                rgt = jnp.where(at_right, side_right, right[4])
                before = pltpu.roll(w, 2, 0) << 1
                after = srl(pltpu.roll(w, 6, 0), 1)
            up = jnp.where(up_prev, before, jnp.where(up_self, w, pltpu.roll(w, 1, 0)))
            down = jnp.where(down_next, after, jnp.where(down_self, w, pltpu.roll(w, 7, 0)))
            lft, rgt, up, down = lft ^ s, rgt ^ s, up ^ s, down ^ s
            s1, c1 = lft ^ rgt, lft & rgt
            s2, c2 = up ^ down, up & down
            k0 = s1 ^ s2
            k1 = (c1 ^ c2) | (s1 & s2)
            k2 = c1 & c2
            k01 = k0 & k1
            if q in (1, 2):
                x = [accept[q - 1, c, t, n] for n in range(LEVELS)]
                flip = x[0] ^ (k0 & x[1]) ^ (k1 & x[2]) ^ (k01 & x[3]) ^ (k2 & x[4])
                new[q] = s ^ flip
                continue
            above = None
            for b in range(8):
                x = [table[b, n] for n in range(LEVELS)]
                limit = x[0] ^ (k0 & x[1]) ^ (k1 & x[2]) ^ (k01 & x[3]) ^ (k2 & x[4])
                if q == 4:
                    u = srl(side_planes[8 * at + b], 8 * p + 4 * c)
                elif joined:
                    u = edge1[c, 8 * at + b]
                else:
                    u = edge0[edge_at[q], c, 8 * at + b]
                above = u & ~limit if above is None else above ^ ((u ^ limit) & (above ^ u))
            new[q] = ~(s ^ above)
        return new

    a, b = ({q: colour[q] for q in range(5)} for colour in state)
    for t in range(SWEEPS):
        if t == 4:
            a[0] = jnp.where(even, a[3], a[0])
            b[0] = jnp.where(odd, b[3], b[0])
        a = half_sweep(a, b, 0, t)
        b = half_sweep(b, a, 1, t)

    copies = []
    tiles = []
    for q in (1, 2):
        first = jnp.where(even, a[q], b[q])
        second = pltpu.roll(jnp.where(even, b[q], a[q]), 1, 0)
        for n, word in enumerate((first, second)):
            row = 16 * (q - 1) + 8 * n
            for g in range(GROUPS):
                spins[pl.ds(row, 8), pl.ds(g * LANES, LANES)] = ((word << (31 - g)) >> 31) | 1
            at = pl.ds(row, 8)
            copies.append(pltpu.make_async_copy(spins.at[at], final.at[at], sems.at[len(copies)]))
            copies[-1].start()
            tiles.append((row, word))
    sums = jnp.zeros((8, LANES), jnp.float32)
    for row, word in tiles:
        minus = jnp.sum(lax.population_count(word).astype(jnp.float32), axis=1, keepdims=True)
        mean = (GROUPS * LANES - 2.0 * minus) * (1.0 / (4 * GROUPS * LANES))
        sums = sums + jnp.where(lane == row + sub, mean, 0.0)
    means[...] = jnp.sum(sums, axis=0, keepdims=True)[:, :32]
    for copy in copies:
        copy.wait()


def rows_are_even():
    return lax.axis_index("rows") % 2 == 0


def cols_are_even():
    return lax.axis_index("cols") % 2 == 0


def side_kernel(lattice, draws, to_partner, to_other, tiles, sem):
    lane = lax.broadcasted_iota(I32, (8, LANES), 1)
    last = (GROUPS - 1) * LANES
    copies = []
    for side, is_last in enumerate((jnp.logical_not(cols_are_even()), cols_are_even())):
        column = pl.ds(pl.multiple_of(jnp.where(is_last, last, 0), LANES), LANES)
        for n, ref in enumerate((lattice, draws.at[0], draws.at[1])):
            target = tiles.at[side, pl.ds(32 * n, 32), :]
            copies.append(pltpu.make_async_copy(ref.at[:, column], target, sem.at[len(copies)]))
            copies[-1].start()
    for copy in copies:
        copy.wait()
    for side, target, is_last in ((0, to_other, jnp.logical_not(cols_are_even())), (1, to_partner, cols_are_even())):
        skip = jnp.where(is_last, 16, 0)
        packed = [jnp.zeros((8, LANES), I32)] * 2
        for k in range(12):
            moved = pltpu.roll(tiles[side, pl.ds(8 * k, 8), :], (16 * (k % 8) + skip) % LANES, 1)
            packed[k // 8] = jnp.where(lane // 16 == k % 8, moved, packed[k // 8])
        target[pl.ds(0, 8), :], target[pl.ds(8, 8), :] = packed


def rows_kernel(lattice, draws, from_partner, from_other, side, near, far):
    lane = lax.broadcasted_iota(I32, (8, LANES), 1)
    partner_is_right = cols_are_even()
    low = (lane < LANES // 2) == partner_is_right
    for k in range(12):
        at = pl.ds(8 * (k // 8), 8)
        back = LANES - 16 * (k % 8)
        partner = pltpu.roll(from_partner[at, :], (back + jnp.where(partner_is_right, 0, LANES - 16)) % LANES, 1)
        other = pltpu.roll(from_other[at, :], (back + jnp.where(partner_is_right, LANES - 16, 0)) % LANES, 1)
        side[pl.ds(8 * k, 8), :] = jnp.where(low, partner, other)
    inner = pl.ds(0, GROUPS * LANES)
    outer = pl.ds(GROUPS * LANES, LANES)
    for target, down in ((far, jnp.logical_not(rows_are_even())), (near, rows_are_even())):
        for n, rows, at in ((0, 16, 0), (1, 16, 16), (2, 8, 32)):
            row = pl.multiple_of(jnp.where(down, 32 - rows, 0), 8)
            ref = lattice if n == 0 else draws.at[n - 1]
            target[pl.ds(at, rows), inner] = ref[pl.ds(row, rows), :]
            target[pl.ds(at, rows), outer] = side[pl.ds(pl.multiple_of(32 * n + row, 8), rows), :]


def swap(x, axis, first):
    count = lax.axis_size(axis)
    pairs = [(i, (i + 1) % count) for i in range(first, count, 2)]
    return lax.ppermute(x, axis, pairs + [(j, i) for i, j in pairs])


def on_device(lattice, draws, thresholds):
    width = GROUPS * LANES
    vmem, smem = pl.BlockSpec(memory_space=pltpu.VMEM), pl.BlockSpec(memory_space=pltpu.SMEM)

    def call(kernel, out_shape, flops, args, **kwargs):
        return pl.pallas_call(
            kernel,
            out_shape=out_shape,
            compiler_params=pltpu.CompilerParams(vmem_limit_bytes=16 << 20),
            cost_estimate=pl.CostEstimate(flops=flops, bytes_accessed=2_000_000, transcendentals=0),
            **kwargs,
        )(*args)

    def words(*shape):
        return jax.ShapeDtypeStruct(shape, I32)

    to_partner, to_other = call(
        side_kernel,
        (words(16, LANES),) * 2,
        1_000_000,
        tuple(pltpu.with_memory_space_constraint(x, pltpu.HBM) for x in (lattice, draws)),
        in_specs=[pl.BlockSpec(memory_space=pltpu.HBM)] * 2,
        scratch_shapes=[pltpu.VMEM((2, 96, LANES), I32), pltpu.SemaphoreType.DMA((6,))],
    )
    from_other = swap(to_other, "cols", 1)
    from_partner = swap(to_partner, "cols", 0)

    side, to_near, to_far = call(
        rows_kernel,
        (words(96, LANES), words(40, width + LANES), words(40, width + LANES)),
        1_000_000,
        (lattice, draws, from_partner, from_other),
    )
    far = swap(to_far, "rows", 1)
    near = swap(to_near, "rows", 0)

    accept, spins, table = call(
        own_kernel,
        (words(2, 2, SWEEPS, LEVELS, 8, LANES), words(2, 2, 8, LANES), words(8, LEVELS, 8, LANES)),
        50_000_000,
        (thresholds, lattice, draws),
        in_specs=[smem, vmem, vmem],
        scratch_shapes=[pltpu.VMEM((32, 8, LANES), I32), pltpu.VMEM((8, LEVELS, 8, LANES), I32)],
    )

    final, means = call(
        sweep_kernel,
        (words(32, width), jax.ShapeDtypeStruct((1, 32), jnp.float32)),
        40_000_000,
        (near, far, side, spins, accept, table),
        in_specs=[vmem] * 6,
        out_specs=(pl.BlockSpec(memory_space=pltpu.HBM), vmem),
        scratch_shapes=[
            pltpu.VMEM((2, 2, 32, 8, LANES), I32),
            pltpu.VMEM((2, 32, 8, LANES), I32),
            pltpu.VMEM((32, 8, LANES), I32),
            pltpu.VMEM((32, width), I32),
            pltpu.SemaphoreType.DMA((4,)),
        ],
    )
    return final, lax.psum(means, "cols").reshape(32)


def solution(mesh):
    in_specs = (P("rows", "cols"), P(None, "rows", "cols"), P())
    out_specs = (P("rows", "cols"), P("rows"))

    return jax.shard_map(on_device, mesh=mesh, in_specs=in_specs, out_specs=out_specs, check_vma=False)
```

time: 54.9 us -> 55 us (level)
  waiting for transfers between devices: 18.2 us -> 17.3 us
    ppermute x2 -> x0, waiting for transfers between devices: 13.2 us -> none  [shift(): return lax.ppermute(x, axis, [(i, (i + by) % count) for i in range(count)])]
    ppermute x2 -> x4, waiting for transfers between devices: 4.98 us -> 17.3 us  [swap(): return lax.ppermute(x, axis, pairs + [(j, i) for i, j in pairs])]
    ppermute x2 -> x4, starting transfers between devices: 10.7 us -> 22.1 us  [swap(): return lax.ppermute(x, axis, pairs + [(j, i) for i, j in pairs])]
    ppermute x2 -> x0, starting transfers between devices: 10.9 us -> none  [shift(): return lax.ppermute(x, axis, [(i, (i + by) % count) for i in range(count)])]
  transfers between devices with their start and end apart: 4 -> 4, of which waited for: 3 -> 3; matrix products, arithmetic and copies ran while one was open for 0% -> 0% of each run, Pallas kernels for 2% -> 5%
where the time goes in v2:
time: 55 us; the launch traced here: 54.7 us
  starting transfers between devices  22.1 us (40%)
  waiting for transfers between devices  17.3 us (31%)
  blocking collectives  7.91 us (14%)
  Pallas kernels  6.66 us (12%)
  between operations  0.73 us (1%)
    ppermute x4, starting transfers between devices, swap(): return lax.ppermute(x, axis, pairs + [(j, i) for i, j in pairs])  22.1 us
    ppermute x4, waiting for transfers between devices, swap(): return lax.ppermute(x, axis, pairs + [(j, i) for i, j in pairs])  17.3 us
    psum x1, blocking collectives, on_device(): return (final, lax.psum(means, 'cols').reshape(32))  7.91 us
    pallas_call x4, Pallas kernels, call(): pl.pallas_call(kernel, out_shape=out_shape, compiler_params=pltpu.Compile...  6.66 us
  transfers between devices with their start and end apart: 4, of which 3 were waited for; matrix products, arithmetic and copies ran while one was open for 0% of the time, Pallas kernels for 5%

profile of v2, /device:TPU:1, one launch (start us, length us, event | category | flops | bytes accessed | tf_op | source)
XLA Modules:
  0.0 54.7 jit_solution(17555471805443116171)
XLA Ops:
  0.6 0.0 copy-start.1
  0.6 0.0 copy-start
  0.6 1.1 %shard_map.50 = (s32[16,128]{1,0:T(8,128)S(1)}, s32[16,128]{1,0:T(8,128)S(1)}) custom-call(s32[32,4096]{1,0:T(8,128)} %lattice.5, s32[2,32,4096]{2,1,0:T(8,128)} %draws.5), custom_call_target="tpu_custom_call" | custom-call | flops 1000000 | bytes 2000000 | tf_op jit(solution)/shard_map/pallas_call | solution.py:337
  1.7 8.7 %collective-permute-start = (s32[16,128]{1,0:T(8,128)S(1)}, s32[16,128]{1,0:T(8,128)S(1)}, u32[]{:S(2)}, u32[]{:S(2)}) collective-permute-start(s32[16,128]{1,0:T(8,128)S(1)} %get-tuple-element.12), channel_id=1, source_target_pairs={{0,1},{2,3},{1,0},{3,2},{4,5},{6,7},{5,4},{7,6},{8,9},{10,11},{9,8... | collective-permute-start | bytes 24584 | tf_op jit(solution)/shard_map/ppermute | solution.py:329
  10.5 1.9 %collective-permute-start.1 = (s32[16,128]{1,0:T(8,128)S(1)}, s32[16,128]{1,0:T(8,128)S(1)}, u32[]{:S(2)}, u32[]{:S(2)}) collective-permute-start(s32[16,128]{1,0:T(8,128)S(1)} %get-tuple-element.13), channel_id=1, source_target_pairs={{1,2},{3,0},{2,1},{0,3},{5,6},{7,4},{6,5},{4,7},{9,10},{11,8},{10,... | collective-permute-start | bytes 24584 | tf_op jit(solution)/shard_map/ppermute | solution.py:329
  12.4 0.0 collective-permute-done.from_partner
  12.4 4.5 %collective-permute-done.1.from_other = s32[16,128]{1,0:T(8,128)S(1)} collective-permute-done((s32[16,128]{1,0:T(8,128)S(1)}, s32[16,128]{1,0:T(8,128)S(1)}, u32[]{:S(2)}, u32[]{:S(2)}) %collective-permute-start.1) | collective-permute-done | bytes 8224 | tf_op jit(solution)/shard_map/ppermute | solution.py:329
  17.0 0.0 copy-done.1
  17.0 0.0 copy-done
  17.0 0.2 shard_map.51
  17.1 0.0 copy-start.2
  17.1 1.9 %collective-permute-start.2 = (s32[40,4224]{1,0:T(8,128)S(1)}, s32[40,4224]{1,0:T(8,128)S(1)}, u32[]{:S(2)}, u32[]{:S(2)}) collective-permute-start(s32[40,4224]{1,0:T(8,128)S(1)} %get-tuple-element.14), channel_id=1, source_target_pairs={{0,4},{8,12},{16,20},{24,28},{32,36},{40,44},{48,52},{56,60},{64,6... | collective-permute-start | bytes 2027528 | tf_op jit(solution)/shard_map/ppermute | solution.py:329
  19.1 9.5 %collective-permute-start.3 = (s32[40,4224]{1,0:T(8,128)S(1)}, s32[40,4224]{1,0:T(8,128)S(1)}, u32[]{:S(2)}, u32[]{:S(2)}) collective-permute-start(s32[40,4224]{1,0:T(8,128)S(1)} %get-tuple-element.15), channel_id=1, source_target_pairs={{4,8},{12,16},{20,24},{28,32},{36,40},{44,48},{52,56},{60,64},{68,... | collective-permute-start | bytes 2027528 | tf_op jit(solution)/shard_map/ppermute | solution.py:329
  28.6 0.0 copy-done.2
  28.6 2.5 %shard_map.52 = (s32[2,2,8,5,8,128]{5,4,3,2,1,0:T(8,128)S(1)}, s32[2,2,8,128]{3,2,1,0:T(8,128)S(1)}, s32[8,5,8,128]{3,2,1,0:T(8,128)S(1)}) custom-call(s32[5]{0:T(128)S(1)} %copy-done.2, s32[32,4096]{1,0:T(8,128)S(1)} %copy-done.1, s32[2,32,4096]{2,1,0:T(8,128)S(1)} %copy-done), custom_call_target="tpu_custom_call" | custom-call | flops 50000000 | bytes 2000000 | tf_op jit(solution)/shard_map/pallas_call | solution.py:337
  31.1 4.7 %collective-permute-done.2.near = s32[40,4224]{1,0:T(8,128)S(1)} collective-permute-done((s32[40,4224]{1,0:T(8,128)S(1)}, s32[40,4224]{1,0:T(8,128)S(1)}, u32[]{:S(2)}, u32[]{:S(2)}) %collective-permute-start.2) | collective-permute-done | bytes 675872 | tf_op jit(solution)/shard_map/ppermute | solution.py:329
  35.7 8.1 %collective-permute-done.3.far = s32[40,4224]{1,0:T(8,128)S(1)} collective-permute-done((s32[40,4224]{1,0:T(8,128)S(1)}, s32[40,4224]{1,0:T(8,128)S(1)}, u32[]{:S(2)}, u32[]{:S(2)}) %collective-permute-start.3) | collective-permute-done | bytes 675872 | tf_op jit(solution)/shard_map/ppermute | solution.py:329
  43.8 3.0 %shard_map.53 = (s32[32,4096]{1,0:T(8,128)}, f32[1,32]{1,0:T(1,128)S(1)}) custom-call(s32[40,4224]{1,0:T(8,128)S(1)} %collective-permute-done.2.near, s32[40,4224]{1,0:T(8,128)S(1)} %collective-permute-done.3.far, s32[96,128]{1,0:T(8,128)S(1)} %get-tuple-element.16.side, s32[2,2,8,128]{3,2,1,0:T(8,128)S(1)} %get-tuple-element.17.words, ...), custom_call_target="tpu_custom_call" | custom-call | flops 40000000 | bytes 2000000 | tf_op jit(solution)/shard_map/pallas_call | solution.py:337
  46.8 7.9 %psum.7 = f32[32]{0:T(128)} all-reduce(f32[32]{0:T(128)S(1)} %bitcast.1), channel_id=1, replica_groups=mesh['rows'=128,'cols'=4] {'cols'}, use_global_device_ids=true, to_apply=%region_0.0 | all-reduce | flops 32 | bytes 256 | tf_op jit(solution)/shard_map/psum | solution.py:392
Async XLA Ops:
  0.6 16.3 %copy-start.1 = (s32[32,4096]{1,0:T(8,128)S(1)}, s32[32,4096]{1,0:T(8,128)}, u32[]{:S(2)}) copy-start(s32[32,4096]{1,0:T(8,128)} %lattice.5) | copy-start | bytes 1572868
  0.6 16.3 %copy-start = (s32[2,32,4096]{2,1,0:T(8,128)S(1)}, s32[2,32,4096]{2,1,0:T(8,128)}, u32[]{:S(2)}) copy-start(s32[2,32,4096]{2,1,0:T(8,128)} %draws.5) | copy-start | bytes 3145732
  1.7 10.7 %collective-permute-start = (s32[16,128]{1,0:T(8,128)S(1)}, s32[16,128]{1,0:T(8,128)S(1)}, u32[]{:S(2)}, u32[]{:S(2)}) collective-permute-start(s32[16,128]{1,0:T(8,128)S(1)} %get-tuple-element.12), channel_id=1, source_target_pairs={{0,1},{2,3},{1,0},{3,2},{4,5},{6,7},{5,4},{7,6},{8,9},{10,11},{9,8... | collective-permute-start | bytes 24584 | tf_op jit(solution)/shard_map/ppermute | solution.py:329
  10.5 6.5 %collective-permute-start.1 = (s32[16,128]{1,0:T(8,128)S(1)}, s32[16,128]{1,0:T(8,128)S(1)}, u32[]{:S(2)}, u32[]{:S(2)}) collective-permute-start(s32[16,128]{1,0:T(8,128)S(1)} %get-tuple-element.13), channel_id=1, source_target_pairs={{1,2},{3,0},{2,1},{0,3},{5,6},{7,4},{6,5},{4,7},{9,10},{11,8},{10,... | collective-permute-start | bytes 24584 | tf_op jit(solution)/shard_map/ppermute | solution.py:329
  17.1 11.5 %copy-start.2 = (s32[5]{0:T(128)S(1)}, s32[5]{0:T(128)}, u32[]{:S(2)}) copy-start(s32[5]{0:T(128)} %thresholds.1) | copy-start | bytes 64
  17.1 18.6 %collective-permute-start.2 = (s32[40,4224]{1,0:T(8,128)S(1)}, s32[40,4224]{1,0:T(8,128)S(1)}, u32[]{:S(2)}, u32[]{:S(2)}) collective-permute-start(s32[40,4224]{1,0:T(8,128)S(1)} %get-tuple-element.14), channel_id=1, source_target_pairs={{0,4},{8,12},{16,20},{24,28},{32,36},{40,44},{48,52},{56,60},{64,6... | collective-permute-start | bytes 2027528 | tf_op jit(solution)/shard_map/ppermute | solution.py:329
  19.1 24.8 %collective-permute-start.3 = (s32[40,4224]{1,0:T(8,128)S(1)}, s32[40,4224]{1,0:T(8,128)S(1)}, u32[]{:S(2)}, u32[]{:S(2)}) collective-permute-start(s32[40,4224]{1,0:T(8,128)S(1)} %get-tuple-element.15), channel_id=1, source_target_pairs={{4,8},{12,16},{20,24},{28,32},{36,40},{44,48},{52,56},{60,64},{68,... | collective-permute-start | bytes 2027528 | tf_op jit(solution)/shard_map/ppermute | solution.py:329

commit v3 on v2

--- a/solution.py
+++ b/solution.py
@@ -113,69 +113,72 @@
 
 
 def sweep_kernel(
-    near, far, side, words, accept, table, final, means, edge0, edge1, side_planes, spins, sems
+    near_top, near, far, side, words, accept, table, final, means, edge0, edge1, side_planes, packed, spins, sems
 ):
     sub, lane, even = iotas()
     odd = jnp.logical_not(even)
 
-    def tile(ref, row, g):
-        return ref[pl.ds(row, 8), pl.ds(g * LANES, LANES)]
-
-    rows_even = rows_are_even()
-
-    def edge_tile(q, row, g):
-        at_near, at_far = tile(near, row, g), tile(far, row, g)
-        return jnp.where(rows_even, at_far, at_near) if q == 0 else jnp.where(rows_even, at_near, at_far)
-
-    def side_tile(q, n, half):
-        if q in (0, 3):
-            return edge_tile(q, (0, 16, 32)[n] + (8 * half if n < 2 else 0), GROUPS)
-        return side[pl.ds(32 * n + 16 * (q - 1) + 8 * half, 8), :]
-
-    state = [[None] * 5, [None] * 5]
-    edges = []
-    for ref in (near, far):
-        first = pack_spins(lambda g: tile(ref, 0, g))
-        second = pack_spins(lambda g: tile(ref, 8, g))
-        edges.append(split_colours(first, second, even))
-    for c in range(2):
-        state[c][0] = jnp.where(rows_even, edges[1][c], edges[0][c])
-        state[c][3] = jnp.where(rows_even, edges[0][c], edges[1][c])
-    for q in (1, 2):
-        for c in range(2):
-            state[c][q] = words[q - 1, c]
-    state[0][4] = state[1][4] = jnp.zeros((8, LANES), I32)
-    for q in range(4):
-        pair = split_colours(side_tile(q, 0, 0), side_tile(q, 0, 1), even)
-        for c in range(2):
-            state[c][4] = state[c][4] | ((srl(pair[c], 1) & 1) << q)
-
-    for n, ref in enumerate((near, far)):
-        pairs = [split_colours(tile(ref, 16, g), tile(ref, 24, g), even) for g in range(GROUPS)]
+    def from_near(row):
+        return near_top[pl.ds(row, 8), :] | near[pl.ds(row, 8), :]
+
+    def from_far(row):
+        return far[pl.ds(row, 8), :]
+
+    def read_edges(top, bot):
+        for n, load in enumerate((top, bot)):
+            first = pack_spins(lambda g: load(DEEP * g))
+            second = pack_spins(lambda g: load(DEEP * g + 8))
+            packed[n, 0], packed[n, 1] = split_colours(first, second, even)
+            at = 15 if n == 0 else 16
+            pairs = [split_colours(load(DEEP * g + at), load(DEEP * g + at + 8), even) for g in range(GROUPS)]
+            for c in range(2):
+                for b, plane in enumerate(transpose_bits([pair[c] for pair in pairs])):
+                    edge0[n, c, b] = plane
+        pairs = [split_colours(bot(DEEP * g + 31), top(DEEP * g + 30), even) for g in range(GROUPS)]
         for c in range(2):
             for b, plane in enumerate(transpose_bits([pair[c] for pair in pairs])):
-                edge0[n, c, b] = plane
-    pairs = [split_colours(edge_tile(3, 32, g), edge_tile(0, 32, g), even) for g in range(GROUPS)]
-    for c in range(2):
-        for b, plane in enumerate(transpose_bits([pair[c] for pair in pairs])):
-            edge1[c, b] = plane
-    slots = [jnp.zeros((8, LANES), I32)] * 32
-    for q in range(4):
-        slots[q], slots[4 + q] = split_colours(side_tile(q, 1, 0), side_tile(q, 1, 1), even)
-        if q in (0, 3):
-            slots[8 + q], slots[12 + q] = split_colours(side_tile(3, 2, 0), side_tile(0, 2, 1), even)
-        else:
-            slots[8 + q], slots[12 + q] = split_colours(side_tile(q, 2, 0), side_tile(q, 2, 1), even)
-    for b, plane in enumerate(transpose_bits(slots, low_half=True)):
-        side_planes[b] = plane
+                edge1[c, b] = plane
+
+        outer = []
+        for load in (top, bot):
+            dense = (load(SIDE_AT), load(SIDE_AT + 8))
+            outer.append([pltpu.roll(dense[k // 4], LANES - 16 - 32 * (k % 4), 1) for k in range(4)])
+            outer[-1].append(pltpu.roll(dense[1], LANES - 16, 1))
+
+        def side_tiles(q, n):
+            if q in (0, 3):
+                return outer[q // 3][2 * n], outer[q // 3][2 * n + 1]
+            at = 32 * n + 16 * (q - 1)
+            return side[pl.ds(at, 8), :], side[pl.ds(at + 8, 8), :]
+
+        columns = [jnp.zeros((8, LANES), I32)] * 2
+        slots = [jnp.zeros((8, LANES), I32)] * 32
+        for q in range(4):
+            pair = split_colours(*side_tiles(q, 0), even)
+            for c in range(2):
+                columns[c] = columns[c] | ((srl(pair[c], 1) & 1) << q)
+            slots[q], slots[4 + q] = split_colours(*side_tiles(q, 1), even)
+            second_word = (outer[1][4], outer[0][4]) if q in (0, 3) else side_tiles(q, 2)
+            slots[8 + q], slots[12 + q] = split_colours(*second_word, even)
+        packed[2, 0], packed[2, 1] = columns
+        for b, plane in enumerate(transpose_bits(slots, low_half=True)):
+            side_planes[b] = plane
+
+    @pl.when(rows_are_even())
+    def _():
+        read_edges(from_far, from_near)
+
+    @pl.when(jnp.logical_not(rows_are_even()))
+    def _():
+        read_edges(from_near, from_far)
+
+    state = [[packed[0, c], words[0, c], words[1, c], packed[1, c], packed[2, c]] for c in range(2)]
 
     at_left, at_right = lane == 0, lane == LANES - 1
     fix = []
     for c in range(2):
         here, there = (even, odd) if c == 0 else (odd, even)
         fix.append((here & (sub == 0), there & (sub == 7), here & (sub == 7), there & (sub == 6)))
-
-    edge_at = {0: jnp.where(rows_even, 1, 0), 3: jnp.where(rows_even, 0, 1)}
 
     def half_sweep(mine, other, c, t):
         p, at = t // 4, t % 4
@@ -238,7 +241,7 @@
                 elif joined:
                     u = edge1[c, 8 * at + b]
                 else:
-                    u = edge0[edge_at[q], c, 8 * at + b]
+                    u = edge0[q // 3, c, 8 * at + b]
                 above = u & ~limit if above is None else above ^ ((u ^ limit) & (above ^ u))
             new[q] = ~(s ^ above)
         return new
@@ -303,6 +306,11 @@
         target[pl.ds(0, 8), :], target[pl.ds(8, 8), :] = packed
 
 
+DEEP = 38
+SIDE_AT = DEEP * GROUPS
+MESSAGE = SIDE_AT + 16
+
+
 def rows_kernel(lattice, draws, from_partner, from_other, side, near, far):
     lane = lax.broadcasted_iota(I32, (8, LANES), 1)
     partner_is_right = cols_are_even()
@@ -313,19 +321,36 @@
         partner = pltpu.roll(from_partner[at, :], (back + jnp.where(partner_is_right, 0, LANES - 16)) % LANES, 1)
         other = pltpu.roll(from_other[at, :], (back + jnp.where(partner_is_right, LANES - 16, 0)) % LANES, 1)
         side[pl.ds(8 * k, 8), :] = jnp.where(low, partner, other)
-    inner = pl.ds(0, GROUPS * LANES)
-    outer = pl.ds(GROUPS * LANES, LANES)
-    for target, down in ((far, jnp.logical_not(rows_are_even())), (near, rows_are_even())):
-        for n, rows, at in ((0, 16, 0), (1, 16, 16), (2, 8, 32)):
-            row = pl.multiple_of(jnp.where(down, 32 - rows, 0), 8)
-            ref = lattice if n == 0 else draws.at[n - 1]
-            target[pl.ds(at, rows), inner] = ref[pl.ds(row, rows), :]
-            target[pl.ds(at, rows), outer] = side[pl.ds(pl.multiple_of(32 * n + row, 8), rows), :]
-
-
-def swap(x, axis, first):
+
+    def write(target, down):
+        below = (((2, 24), 30), ((1, 24), 23), ((1, 16), 15), ((0, 24), 8), ((0, 16), 0))
+        above = (((0, 0), 0), ((0, 8), 8), ((1, 0), 16), ((1, 8), 24), ((2, 0), 31))
+        for g in range(GROUPS):
+            for (n, row), at in below if down else above:
+                ref = lattice if n == 0 else draws.at[n - 1]
+                target[pl.ds(DEEP * g + at, 8), :] = ref[pl.ds(row, 8), pl.ds(g * LANES, LANES)]
+        start = 16 if down else 0
+        dense = jnp.zeros((8, LANES), I32)
+        for k, row in enumerate((start, start + 8, 32 + start, 40 + start, 88 if down else 64)):
+            moved = pltpu.roll(side[pl.ds(row, 8), :], (32 * (k % 4) + 16) % LANES, 1)
+            dense = jnp.where(lane // 32 == k % 4, moved, dense)
+            if k >= 3:
+                target[pl.ds(SIDE_AT + 8 * (k - 3), 8), :] = dense
+
+    @pl.when(rows_are_even())
+    def _():
+        write(near, True)
+        write(far, False)
+
+    @pl.when(jnp.logical_not(rows_are_even()))
+    def _():
+        write(far, True)
+        write(near, False)
+
+
+def swap(x, axis, first, only=None):
     count = lax.axis_size(axis)
-    pairs = [(i, (i + 1) % count) for i in range(first, count, 2)]
+    pairs = [(i, (i + 1) % count) for i in range(first, count, 2)][only or slice(None)]
     return lax.ppermute(x, axis, pairs + [(j, i) for i, j in pairs])
 
 
@@ -358,12 +383,13 @@
 
     side, to_near, to_far = call(
         rows_kernel,
-        (words(96, LANES), words(40, width + LANES), words(40, width + LANES)),
+        (words(96, LANES), words(MESSAGE, LANES), words(MESSAGE, LANES)),
         1_000_000,
         (lattice, draws, from_partner, from_other),
     )
+    near_top = swap(to_near, "rows", 0, slice(0, 1))
     far = swap(to_far, "rows", 1)
-    near = swap(to_near, "rows", 0)
+    near = swap(to_near, "rows", 0, slice(1, None))
 
     accept, spins, table = call(
         own_kernel,
@@ -378,13 +404,14 @@
         sweep_kernel,
         (words(32, width), jax.ShapeDtypeStruct((1, 32), jnp.float32)),
         40_000_000,
-        (near, far, side, spins, accept, table),
-        in_specs=[vmem] * 6,
+        (near_top, near, far, side, spins, accept, table),
+        in_specs=[vmem] * 7,
         out_specs=(pl.BlockSpec(memory_space=pltpu.HBM), vmem),
         scratch_shapes=[
             pltpu.VMEM((2, 2, 32, 8, LANES), I32),
             pltpu.VMEM((2, 32, 8, LANES), I32),
             pltpu.VMEM((32, 8, LANES), I32),
+            pltpu.VMEM((3, 2, 8, LANES), I32),
             pltpu.VMEM((32, width), I32),
             pltpu.SemaphoreType.DMA((4,)),
         ],

time: 55 us -> 55.4 us (level)
  waiting for transfers between devices: 17.3 us -> 16.3 us
  starting transfers between devices: 22.1 us -> 22.9 us
    ppermute x4 -> x5, waiting for transfers between devices: 17.3 us -> 16.3 us  [swap(): return lax.ppermute(x, axis, pairs + [(j, i) for i, j in pairs])]
    ppermute x4 -> x5, starting transfers between devices: 22.1 us -> 22.9 us  [swap(): return lax.ppermute(x, axis, pairs + [(j, i) for i, j in pairs])]
  transfers between devices with their start and end apart: 4 -> 5, of which waited for: 3 -> 3; matrix products, arithmetic and copies ran while one was open for 0% -> 0% of each run, Pallas kernels for 5% -> 4%
where the time goes in v3:
time: 55.4 us; the launch traced here: 55.1 us
  starting transfers between devices  22.9 us (41%)
  waiting for transfers between devices  16.3 us (29%)
  blocking collectives  7.93 us (14%)
  Pallas kernels  7.16 us (13%)
  between operations  0.73 us (1%)
    ppermute x5, starting transfers between devices, swap(): return lax.ppermute(x, axis, pairs + [(j, i) for i, j in pairs])  22.9 us
    ppermute x5, waiting for transfers between devices, swap(): return lax.ppermute(x, axis, pairs + [(j, i) for i, j in pairs])  16.3 us
    psum x1, blocking collectives, on_device(): return (final, lax.psum(means, 'cols').reshape(32))  7.93 us
    pallas_call x4, Pallas kernels, call(): pl.pallas_call(kernel, out_shape=out_shape, compiler_params=pltpu.Compile...  7.16 us
  transfers between devices with their start and end apart: 5, of which 3 were waited for; matrix products, arithmetic and copies ran while one was open for 0% of the time, Pallas kernels for 4%

profile of v3, /device:TPU:1, one launch (start us, length us, event | category | flops | bytes accessed | tf_op | source)
XLA Modules:
  0.0 55.1 jit_solution(15416418628327081763)
XLA Ops:
  0.6 0.0 copy-start.1
  0.6 0.0 copy-start
  0.6 1.1 %shard_map.50 = (s32[16,128]{1,0:T(8,128)S(1)}, s32[16,128]{1,0:T(8,128)S(1)}) custom-call(s32[32,4096]{1,0:T(8,128)} %lattice.5, s32[2,32,4096]{2,1,0:T(8,128)} %draws.5), custom_call_target="tpu_custom_call" | custom-call | flops 1000000 | bytes 2000000 | tf_op jit(solution)/shard_map/pallas_call | solution.py:362
  1.7 8.7 %collective-permute-start = (s32[16,128]{1,0:T(8,128)S(1)}, s32[16,128]{1,0:T(8,128)S(1)}, u32[]{:S(2)}, u32[]{:S(2)}) collective-permute-start(s32[16,128]{1,0:T(8,128)S(1)} %get-tuple-element.12), channel_id=1, source_target_pairs={{0,1},{2,3},{1,0},{3,2},{4,5},{6,7},{5,4},{7,6},{8,9},{10,11},{9,8... | collective-permute-start | bytes 24584 | tf_op jit(solution)/shard_map/ppermute | solution.py:354
  10.5 1.9 %collective-permute-start.1 = (s32[16,128]{1,0:T(8,128)S(1)}, s32[16,128]{1,0:T(8,128)S(1)}, u32[]{:S(2)}, u32[]{:S(2)}) collective-permute-start(s32[16,128]{1,0:T(8,128)S(1)} %get-tuple-element.13), channel_id=1, source_target_pairs={{1,2},{3,0},{2,1},{0,3},{5,6},{7,4},{6,5},{4,7},{9,10},{11,8},{10,... | collective-permute-start | bytes 24584 | tf_op jit(solution)/shard_map/ppermute | solution.py:354
  12.4 0.0 collective-permute-done.from_partner
  12.4 4.5 %collective-permute-done.1.from_other = s32[16,128]{1,0:T(8,128)S(1)} collective-permute-done((s32[16,128]{1,0:T(8,128)S(1)}, s32[16,128]{1,0:T(8,128)S(1)}, u32[]{:S(2)}, u32[]{:S(2)}) %collective-permute-start.1) | collective-permute-done | bytes 8224 | tf_op jit(solution)/shard_map/ppermute | solution.py:354
  17.0 0.0 copy-done.1
  17.0 0.0 copy-done
  17.0 0.2 shard_map.51
  17.2 0.0 copy-start.2
  17.2 2.1 %collective-permute-start.2 = (s32[1232,128]{1,0:T(8,128)S(1)}, s32[1232,128]{1,0:T(8,128)S(1)}, u32[]{:S(2)}, u32[]{:S(2)}) collective-permute-start(s32[1232,128]{1,0:T(8,128)S(1)} %get-tuple-element.14), channel_id=1, source_target_pairs={{0,4},{4,0},{1,5},{5,1},{2,6},{6,2},{3,7},{7,3}} | collective-permute-start | bytes 1892360 | tf_op jit(solution)/shard_map/ppermute | solution.py:354
  19.2 0.7 %collective-permute-start.3 = (s32[1232,128]{1,0:T(8,128)S(1)}, s32[1232,128]{1,0:T(8,128)S(1)}, u32[]{:S(2)}, u32[]{:S(2)}) collective-permute-start(s32[1232,128]{1,0:T(8,128)S(1)} %get-tuple-element.14), channel_id=1, source_target_pairs={{8,12},{16,20},{24,28},{32,36},{40,44},{48,52},{56,60},{64,68},{72... | collective-permute-start | bytes 1892360 | tf_op jit(solution)/shard_map/ppermute | solution.py:354
  19.9 9.5 %collective-permute-start.4 = (s32[1232,128]{1,0:T(8,128)S(1)}, s32[1232,128]{1,0:T(8,128)S(1)}, u32[]{:S(2)}, u32[]{:S(2)}) collective-permute-start(s32[1232,128]{1,0:T(8,128)S(1)} %get-tuple-element.15), channel_id=1, source_target_pairs={{4,8},{12,16},{20,24},{28,32},{36,40},{44,48},{52,56},{60,64},{68,... | collective-permute-start | bytes 1892360 | tf_op jit(solution)/shard_map/ppermute | solution.py:354
  29.5 0.0 copy-done.2
  29.5 2.5 %shard_map.52 = (s32[2,2,8,5,8,128]{5,4,3,2,1,0:T(8,128)S(1)}, s32[2,2,8,128]{3,2,1,0:T(8,128)S(1)}, s32[8,5,8,128]{3,2,1,0:T(8,128)S(1)}) custom-call(s32[5]{0:T(128)S(1)} %copy-done.2, s32[32,4096]{1,0:T(8,128)S(1)} %copy-done.1, s32[2,32,4096]{2,1,0:T(8,128)S(1)} %copy-done), custom_call_target="tpu_custom_call" | custom-call | flops 50000000 | bytes 2000000 | tf_op jit(solution)/shard_map/pallas_call | solution.py:362
  32.0 3.0 %collective-permute-done.2.near_top = s32[1232,128]{1,0:T(8,128)S(1)} collective-permute-done((s32[1232,128]{1,0:T(8,128)S(1)}, s32[1232,128]{1,0:T(8,128)S(1)}, u32[]{:S(2)}, u32[]{:S(2)}) %collective-permute-start.2) | collective-permute-done | bytes 630816 | tf_op jit(solution)/shard_map/ppermute | solution.py:354
  34.9 0.0 collective-permute-done.3.near
  35.0 8.8 %collective-permute-done.4.far = s32[1232,128]{1,0:T(8,128)S(1)} collective-permute-done((s32[1232,128]{1,0:T(8,128)S(1)}, s32[1232,128]{1,0:T(8,128)S(1)}, u32[]{:S(2)}, u32[]{:S(2)}) %collective-permute-start.4) | collective-permute-done | bytes 630816 | tf_op jit(solution)/shard_map/ppermute | solution.py:354
  43.7 3.4 %shard_map.53 = (s32[32,4096]{1,0:T(8,128)}, f32[1,32]{1,0:T(1,128)S(1)}) custom-call(s32[1232,128]{1,0:T(8,128)S(1)} %collective-permute-done.2.near_top, s32[1232,128]{1,0:T(8,128)S(1)} %collective-permute-done.3.near, s32[1232,128]{1,0:T(8,128)S(1)} %collective-permute-done.4.far, s32[96,128]{1,0:T(8,128)S(1)} %get-tuple-element.16.side, ...), custom_call_target="tpu_custom_call" | custom-call | flops 40000000 | bytes 2000000 | tf_op jit(solution)/shard_map/pallas_call | solution.py:362
  47.2 7.9 %psum.7 = f32[32]{0:T(128)} all-reduce(f32[32]{0:T(128)S(1)} %bitcast.1), channel_id=1, replica_groups=mesh['rows'=128,'cols'=4] {'cols'}, use_global_device_ids=true, to_apply=%region_0.0 | all-reduce | flops 32 | bytes 256 | tf_op jit(solution)/shard_map/psum | solution.py:419
Async XLA Ops:
  0.6 16.3 %copy-start.1 = (s32[32,4096]{1,0:T(8,128)S(1)}, s32[32,4096]{1,0:T(8,128)}, u32[]{:S(2)}) copy-start(s32[32,4096]{1,0:T(8,128)} %lattice.5) | copy-start | bytes 1572868
  0.6 16.3 %copy-start = (s32[2,32,4096]{2,1,0:T(8,128)S(1)}, s32[2,32,4096]{2,1,0:T(8,128)}, u32[]{:S(2)}) copy-start(s32[2,32,4096]{2,1,0:T(8,128)} %draws.5) | copy-start | bytes 3145732
  1.7 10.7 %collective-permute-start = (s32[16,128]{1,0:T(8,128)S(1)}, s32[16,128]{1,0:T(8,128)S(1)}, u32[]{:S(2)}, u32[]{:S(2)}) collective-permute-start(s32[16,128]{1,0:T(8,128)S(1)} %get-tuple-element.12), channel_id=1, source_target_pairs={{0,1},{2,3},{1,0},{3,2},{4,5},{6,7},{5,4},{7,6},{8,9},{10,11},{9,8... | collective-permute-start | bytes 24584 | tf_op jit(solution)/shard_map/ppermute | solution.py:354
  10.5 6.5 %collective-permute-start.1 = (s32[16,128]{1,0:T(8,128)S(1)}, s32[16,128]{1,0:T(8,128)S(1)}, u32[]{:S(2)}, u32[]{:S(2)}) collective-permute-start(s32[16,128]{1,0:T(8,128)S(1)} %get-tuple-element.13), channel_id=1, source_target_pairs={{1,2},{3,0},{2,1},{0,3},{5,6},{7,4},{6,5},{4,7},{9,10},{11,8},{10,... | collective-permute-start | bytes 24584 | tf_op jit(solution)/shard_map/ppermute | solution.py:354
  17.2 12.3 %copy-start.2 = (s32[5]{0:T(128)S(1)}, s32[5]{0:T(128)}, u32[]{:S(2)}) copy-start(s32[5]{0:T(128)} %thresholds.1) | copy-start | bytes 64
  17.2 17.8 %collective-permute-start.2 = (s32[1232,128]{1,0:T(8,128)S(1)}, s32[1232,128]{1,0:T(8,128)S(1)}, u32[]{:S(2)}, u32[]{:S(2)}) collective-permute-start(s32[1232,128]{1,0:T(8,128)S(1)} %get-tuple-element.14), channel_id=1, source_target_pairs={{0,4},{4,0},{1,5},{5,1},{2,6},{6,2},{3,7},{7,3}} | collective-permute-start | bytes 1892360 | tf_op jit(solution)/shard_map/ppermute | solution.py:354
  19.2 15.7 %collective-permute-start.3 = (s32[1232,128]{1,0:T(8,128)S(1)}, s32[1232,128]{1,0:T(8,128)S(1)}, u32[]{:S(2)}, u32[]{:S(2)}) collective-permute-start(s32[1232,128]{1,0:T(8,128)S(1)} %get-tuple-element.14), channel_id=1, source_target_pairs={{8,12},{16,20},{24,28},{32,36},{40,44},{48,52},{56,60},{64,68},{72... | collective-permute-start | bytes 1892360 | tf_op jit(solution)/shard_map/ppermute | solution.py:354
  19.9 23.8 %collective-permute-start.4 = (s32[1232,128]{1,0:T(8,128)S(1)}, s32[1232,128]{1,0:T(8,128)S(1)}, u32[]{:S(2)}, u32[]{:S(2)}) collective-permute-start(s32[1232,128]{1,0:T(8,128)S(1)} %get-tuple-element.15), channel_id=1, source_target_pairs={{4,8},{12,16},{20,24},{28,32},{36,40},{44,48},{52,56},{60,64},{68,... | collective-permute-start | bytes 1892360 | tf_op jit(solution)/shard_map/ppermute | solution.py:354

commit v4 on v3

--- a/solution.py
+++ b/solution.py
@@ -57,17 +57,24 @@
     return word
 
 
-def own_kernel(thresholds, lattice, draws, accept, words, table, planes, clears):
+def acceptance(u, table):
+    r = []
+    for k in range(LEVELS):
+        z = table[0, 0, k]
+        for b in range(8):
+            z = (z & (u[b] ^ table[0, b, k])) ^ table[1, b, k]
+        r.append(z)
+    return r
+
+
+def own_kernel(thresholds, lattice, draws, accept, words, table, planes):
     _, _, even = iotas()
 
-    bits = [[-(((thresholds[LEVELS - 1 - k] - 1) >> b) & 1) for b in range(8)] for k in range(LEVELS)]
-    for b in range(8):
-        r = [bits[k][b] for k in range(LEVELS)]
-        forms = (r[0], r[0] ^ r[1], r[0] ^ r[2], r[0] ^ r[1] ^ r[2] ^ r[3], r[0] ^ r[4])
-        for n, form in enumerate(forms):
-            table[b, n] = jnp.full((8, LANES), form, I32)
-        for k in range(LEVELS):
-            clears[b, k] = jnp.full((8, LANES), ~bits[k][b], I32)
+    for k in range(LEVELS):
+        clear = [((thresholds[LEVELS - 1 - k] - 1) >> b & 1) - 1 for b in range(8)]
+        for b in range(8):
+            table[0, b, k] = jnp.full((8, LANES), clear[b], I32)
+            table[1, b, k] = jnp.full((8, LANES), clear[b] ^ (clear[b + 1] if b < 7 else -1), I32)
 
     def tile(ref, row, g):
         return ref[pl.ds(row, 8), pl.ds(g * LANES, LANES)]
@@ -90,21 +97,9 @@
 
         def one_sweep(t, carry):
             u = [planes[8 * t + b] for b in range(8)]
-            below = []
-            for k in range(LEVELS):
-                clear = [clears[b, k] for b in range(8)]
-                z = clear[0]
-                for b in range(8):
-                    z = z & (u[b] ^ clear[b])
-                    z = ~(z ^ clear[b]) if b == 7 else z ^ (clear[b] ^ clear[b + 1])
-                below.append(z)
-            r = below
             at = 4 * p + t
-            accept[q, c, at, 0] = r[0]
-            accept[q, c, at, 1] = r[0] ^ r[1]
-            accept[q, c, at, 2] = r[0] ^ r[2]
-            accept[q, c, at, 3] = r[0] ^ r[1] ^ r[2] ^ r[3]
-            accept[q, c, at, 4] = r[0] ^ r[4]
+            for n, form in enumerate(acceptance(u, table)):
+                accept[q, c, at, n] = form
             return carry
 
         return lax.fori_loop(0, 4, one_sweep, carry)
@@ -180,8 +175,26 @@
         here, there = (even, odd) if c == 0 else (odd, even)
         fix.append((here & (sub == 0), there & (sub == 7), here & (sub == 7), there & (sub == 6)))
 
-    def half_sweep(mine, other, c, t):
+    def rules_of(c, t):
         p, at = t // 4, t % 4
+        joined = p == 1
+        blocks = (0, 1, 2, 4) if joined else (0, 1, 2, 3, 4)
+        rules = {}
+        for q in blocks:
+            if q in (1, 2):
+                rules[q] = [accept[q - 1, c, t, n] for n in range(LEVELS)]
+                continue
+            if q == 4:
+                u = [srl(side_planes[8 * at + b], 8 * p + 4 * c) for b in range(8)]
+            elif joined:
+                u = [edge1[c, 8 * at + b] for b in range(8)]
+            else:
+                u = [edge0[q // 3, c, 8 * at + b] for b in range(8)]
+            rules[q] = acceptance(u, table)
+        return rules
+
+    def half_sweep(mine, other, c, t, rules):
+        p = t // 4
         joined = p == 1
         blocks = (0, 1, 2, 4) if joined else (0, 1, 2, 3, 4)
         up_prev, up_self, down_self, down_next = fix[c]
@@ -221,38 +234,25 @@
             up = jnp.where(up_prev, before, jnp.where(up_self, w, pltpu.roll(w, 1, 0)))
             down = jnp.where(down_next, after, jnp.where(down_self, w, pltpu.roll(w, 7, 0)))
             lft, rgt, up, down = lft ^ s, rgt ^ s, up ^ s, down ^ s
-            s1, c1 = lft ^ rgt, lft & rgt
-            s2, c2 = up ^ down, up & down
-            k0 = s1 ^ s2
-            k1 = (c1 ^ c2) | (s1 & s2)
-            k2 = c1 & c2
-            k01 = k0 & k1
-            if q in (1, 2):
-                x = [accept[q - 1, c, t, n] for n in range(LEVELS)]
-                flip = x[0] ^ (k0 & x[1]) ^ (k1 & x[2]) ^ (k01 & x[3]) ^ (k2 & x[4])
-                new[q] = s ^ flip
-                continue
-            above = None
-            for b in range(8):
-                x = [table[b, n] for n in range(LEVELS)]
-                limit = x[0] ^ (k0 & x[1]) ^ (k1 & x[2]) ^ (k01 & x[3]) ^ (k2 & x[4])
-                if q == 4:
-                    u = srl(side_planes[8 * at + b], 8 * p + 4 * c)
-                elif joined:
-                    u = edge1[c, 8 * at + b]
-                else:
-                    u = edge0[q // 3, c, 8 * at + b]
-                above = u & ~limit if above is None else above ^ ((u ^ limit) & (above ^ u))
-            new[q] = ~(s ^ above)
+            r = rules[q]
+            one, two = up ^ down, up & down
+            with_none = r[0] ^ (one & (r[0] ^ r[1])) ^ (two & (r[0] ^ r[2]))
+            with_one = r[1] ^ (one & (r[1] ^ r[2])) ^ (two & (r[1] ^ r[3]))
+            with_two = r[2] ^ (one & (r[2] ^ r[3])) ^ (two & (r[2] ^ r[4]))
+            keep = s ^ with_none
+            new[q] = keep ^ ((lft ^ rgt) & (with_none ^ with_one)) ^ ((lft & rgt) & (with_none ^ with_two))
         return new
 
     a, b = ({q: colour[q] for q in range(5)} for colour in state)
+    rules = rules_of(0, 0)
     for t in range(SWEEPS):
         if t == 4:
             a[0] = jnp.where(even, a[3], a[0])
             b[0] = jnp.where(odd, b[3], b[0])
-        a = half_sweep(a, b, 0, t)
-        b = half_sweep(b, a, 1, t)
+        after = rules_of(1, t)
+        a = half_sweep(a, b, 0, t, rules)
+        rules = rules_of(0, t + 1) if t < SWEEPS - 1 else None
+        b = half_sweep(b, a, 1, t, after)
 
     copies = []
     tiles = []
@@ -393,11 +393,11 @@
 
     accept, spins, table = call(
         own_kernel,
-        (words(2, 2, SWEEPS, LEVELS, 8, LANES), words(2, 2, 8, LANES), words(8, LEVELS, 8, LANES)),
+        (words(2, 2, SWEEPS, LEVELS, 8, LANES), words(2, 2, 8, LANES), words(2, 8, LEVELS, 8, LANES)),
         50_000_000,
         (thresholds, lattice, draws),
         in_specs=[smem, vmem, vmem],
-        scratch_shapes=[pltpu.VMEM((32, 8, LANES), I32), pltpu.VMEM((8, LEVELS, 8, LANES), I32)],
+        scratch_shapes=[pltpu.VMEM((32, 8, LANES), I32)],
     )
 
     final, means = call(

time: 55.4 us -> 54.7 us (0.987)
  Pallas kernels: 7.16 us -> 6.41 us
    pallas_call x4, Pallas kernels: 7.16 us -> 6.41 us  [call(): pl.pallas_call(kernel, out_shape=out_shape, compiler_params=pltpu.Compile...]
where the time goes in v4:
time: 54.7 us; the launch traced here: 54.5 us
  starting transfers between devices  22.9 us (42%)
  waiting for transfers between devices  16.5 us (30%)
  blocking collectives  7.9 us (14%)
  Pallas kernels  6.41 us (12%)
  between operations  0.73 us (1%)
    ppermute x5, starting transfers between devices, swap(): return lax.ppermute(x, axis, pairs + [(j, i) for i, j in pairs])  22.9 us
    ppermute x5, waiting for transfers between devices, swap(): return lax.ppermute(x, axis, pairs + [(j, i) for i, j in pairs])  16.5 us
    psum x1, blocking collectives, on_device(): return (final, lax.psum(means, 'cols').reshape(32))  7.9 us
    pallas_call x4, Pallas kernels, call(): pl.pallas_call(kernel, out_shape=out_shape, compiler_params=pltpu.Compile...  6.41 us
  transfers between devices with their start and end apart: 5, of which 3 were waited for; matrix products, arithmetic and copies ran while one was open for 0% of the time, Pallas kernels for 4%

profile of v4, /device:TPU:1, one launch (start us, length us, event | category | flops | bytes accessed | tf_op | source)
XLA Modules:
  0.0 54.5 jit_solution(11414297289156895006)
XLA Ops:
  0.6 0.0 copy-start.1
  0.6 0.0 copy-start
  0.6 1.1 %shard_map.50 = (s32[16,128]{1,0:T(8,128)S(1)}, s32[16,128]{1,0:T(8,128)S(1)}) custom-call(s32[32,4096]{1,0:T(8,128)} %lattice.5, s32[2,32,4096]{2,1,0:T(8,128)} %draws.5), custom_call_target="tpu_custom_call" | custom-call | flops 1000000 | bytes 2000000 | tf_op jit(solution)/shard_map/pallas_call | solution.py:362
  1.7 8.7 %collective-permute-start = (s32[16,128]{1,0:T(8,128)S(1)}, s32[16,128]{1,0:T(8,128)S(1)}, u32[]{:S(2)}, u32[]{:S(2)}) collective-permute-start(s32[16,128]{1,0:T(8,128)S(1)} %get-tuple-element.12), channel_id=1, source_target_pairs={{0,1},{2,3},{1,0},{3,2},{4,5},{6,7},{5,4},{7,6},{8,9},{10,11},{9,8... | collective-permute-start | bytes 24584 | tf_op jit(solution)/shard_map/ppermute | solution.py:354
  10.5 1.9 %collective-permute-start.1 = (s32[16,128]{1,0:T(8,128)S(1)}, s32[16,128]{1,0:T(8,128)S(1)}, u32[]{:S(2)}, u32[]{:S(2)}) collective-permute-start(s32[16,128]{1,0:T(8,128)S(1)} %get-tuple-element.13), channel_id=1, source_target_pairs={{1,2},{3,0},{2,1},{0,3},{5,6},{7,4},{6,5},{4,7},{9,10},{11,8},{10,... | collective-permute-start | bytes 24584 | tf_op jit(solution)/shard_map/ppermute | solution.py:354
  12.4 0.0 collective-permute-done.from_partner
  12.4 4.5 %collective-permute-done.1.from_other = s32[16,128]{1,0:T(8,128)S(1)} collective-permute-done((s32[16,128]{1,0:T(8,128)S(1)}, s32[16,128]{1,0:T(8,128)S(1)}, u32[]{:S(2)}, u32[]{:S(2)}) %collective-permute-start.1) | collective-permute-done | bytes 8224 | tf_op jit(solution)/shard_map/ppermute | solution.py:354
  17.0 0.0 copy-done.1
  17.0 0.0 copy-done
  17.0 0.2 shard_map.51
  17.2 0.0 copy-start.2
  17.2 2.1 %collective-permute-start.2 = (s32[1232,128]{1,0:T(8,128)S(1)}, s32[1232,128]{1,0:T(8,128)S(1)}, u32[]{:S(2)}, u32[]{:S(2)}) collective-permute-start(s32[1232,128]{1,0:T(8,128)S(1)} %get-tuple-element.14), channel_id=1, source_target_pairs={{0,4},{4,0},{1,5},{5,1},{2,6},{6,2},{3,7},{7,3}} | collective-permute-start | bytes 1892360 | tf_op jit(solution)/shard_map/ppermute | solution.py:354
  19.2 0.7 %collective-permute-start.3 = (s32[1232,128]{1,0:T(8,128)S(1)}, s32[1232,128]{1,0:T(8,128)S(1)}, u32[]{:S(2)}, u32[]{:S(2)}) collective-permute-start(s32[1232,128]{1,0:T(8,128)S(1)} %get-tuple-element.14), channel_id=1, source_target_pairs={{8,12},{16,20},{24,28},{32,36},{40,44},{48,52},{56,60},{64,68},{72... | collective-permute-start | bytes 1892360 | tf_op jit(solution)/shard_map/ppermute | solution.py:354
  19.9 9.5 %collective-permute-start.4 = (s32[1232,128]{1,0:T(8,128)S(1)}, s32[1232,128]{1,0:T(8,128)S(1)}, u32[]{:S(2)}, u32[]{:S(2)}) collective-permute-start(s32[1232,128]{1,0:T(8,128)S(1)} %get-tuple-element.15), channel_id=1, source_target_pairs={{4,8},{12,16},{20,24},{28,32},{36,40},{44,48},{52,56},{60,64},{68,... | collective-permute-start | bytes 1892360 | tf_op jit(solution)/shard_map/ppermute | solution.py:354
  29.5 0.0 copy-done.2
  29.5 2.3 %shard_map.52 = (s32[2,2,8,5,8,128]{5,4,3,2,1,0:T(8,128)S(1)}, s32[2,2,8,128]{3,2,1,0:T(8,128)S(1)}, s32[2,8,5,8,128]{4,3,2,1,0:T(8,128)S(1)}) custom-call(s32[5]{0:T(128)S(1)} %copy-done.2, s32[32,4096]{1,0:T(8,128)S(1)} %copy-done.1, s32[2,32,4096]{2,1,0:T(8,128)S(1)} %copy-done), custom_call_target="tpu_custom_call" | custom-call | flops 50000000 | bytes 2000000 | tf_op jit(solution)/shard_map/pallas_call | solution.py:362
  31.8 3.1 %collective-permute-done.2.near_top = s32[1232,128]{1,0:T(8,128)S(1)} collective-permute-done((s32[1232,128]{1,0:T(8,128)S(1)}, s32[1232,128]{1,0:T(8,128)S(1)}, u32[]{:S(2)}, u32[]{:S(2)}) %collective-permute-start.2) | collective-permute-done | bytes 630816 | tf_op jit(solution)/shard_map/ppermute | solution.py:354
  34.9 0.0 collective-permute-done.3.near
  35.0 8.8 %collective-permute-done.4.far = s32[1232,128]{1,0:T(8,128)S(1)} collective-permute-done((s32[1232,128]{1,0:T(8,128)S(1)}, s32[1232,128]{1,0:T(8,128)S(1)}, u32[]{:S(2)}, u32[]{:S(2)}) %collective-permute-start.4) | collective-permute-done | bytes 630816 | tf_op jit(solution)/shard_map/ppermute | solution.py:354
  43.7 2.8 %shard_map.53 = (s32[32,4096]{1,0:T(8,128)}, f32[1,32]{1,0:T(1,128)S(1)}) custom-call(s32[1232,128]{1,0:T(8,128)S(1)} %collective-permute-done.2.near_top, s32[1232,128]{1,0:T(8,128)S(1)} %collective-permute-done.3.near, s32[1232,128]{1,0:T(8,128)S(1)} %collective-permute-done.4.far, s32[96,128]{1,0:T(8,128)S(1)} %get-tuple-element.16.side, ...), custom_call_target="tpu_custom_call" | custom-call | flops 40000000 | bytes 2000000 | tf_op jit(solution)/shard_map/pallas_call | solution.py:362
  46.6 7.9 %psum.7 = f32[32]{0:T(128)} all-reduce(f32[32]{0:T(128)S(1)} %bitcast.1), channel_id=1, replica_groups=mesh['rows'=128,'cols'=4] {'cols'}, use_global_device_ids=true, to_apply=%region_0.0 | all-reduce | flops 32 | bytes 256 | tf_op jit(solution)/shard_map/psum | solution.py:419
Async XLA Ops:
  0.6 16.3 %copy-start.1 = (s32[32,4096]{1,0:T(8,128)S(1)}, s32[32,4096]{1,0:T(8,128)}, u32[]{:S(2)}) copy-start(s32[32,4096]{1,0:T(8,128)} %lattice.5) | copy-start | bytes 1572868
  0.6 16.3 %copy-start = (s32[2,32,4096]{2,1,0:T(8,128)S(1)}, s32[2,32,4096]{2,1,0:T(8,128)}, u32[]{:S(2)}) copy-start(s32[2,32,4096]{2,1,0:T(8,128)} %draws.5) | copy-start | bytes 3145732
  1.7 10.7 %collective-permute-start = (s32[16,128]{1,0:T(8,128)S(1)}, s32[16,128]{1,0:T(8,128)S(1)}, u32[]{:S(2)}, u32[]{:S(2)}) collective-permute-start(s32[16,128]{1,0:T(8,128)S(1)} %get-tuple-element.12), channel_id=1, source_target_pairs={{0,1},{2,3},{1,0},{3,2},{4,5},{6,7},{5,4},{7,6},{8,9},{10,11},{9,8... | collective-permute-start | bytes 24584 | tf_op jit(solution)/shard_map/ppermute | solution.py:354
  10.5 6.5 %collective-permute-start.1 = (s32[16,128]{1,0:T(8,128)S(1)}, s32[16,128]{1,0:T(8,128)S(1)}, u32[]{:S(2)}, u32[]{:S(2)}) collective-permute-start(s32[16,128]{1,0:T(8,128)S(1)} %get-tuple-element.13), channel_id=1, source_target_pairs={{1,2},{3,0},{2,1},{0,3},{5,6},{7,4},{6,5},{4,7},{9,10},{11,8},{10,... | collective-permute-start | bytes 24584 | tf_op jit(solution)/shard_map/ppermute | solution.py:354
  17.2 12.3 %copy-start.2 = (s32[5]{0:T(128)S(1)}, s32[5]{0:T(128)}, u32[]{:S(2)}) copy-start(s32[5]{0:T(128)} %thresholds.1) | copy-start | bytes 64
  17.2 17.8 %collective-permute-start.2 = (s32[1232,128]{1,0:T(8,128)S(1)}, s32[1232,128]{1,0:T(8,128)S(1)}, u32[]{:S(2)}, u32[]{:S(2)}) collective-permute-start(s32[1232,128]{1,0:T(8,128)S(1)} %get-tuple-element.14), channel_id=1, source_target_pairs={{0,4},{4,0},{1,5},{5,1},{2,6},{6,2},{3,7},{7,3}} | collective-permute-start | bytes 1892360 | tf_op jit(solution)/shard_map/ppermute | solution.py:354
  19.2 15.7 %collective-permute-start.3 = (s32[1232,128]{1,0:T(8,128)S(1)}, s32[1232,128]{1,0:T(8,128)S(1)}, u32[]{:S(2)}, u32[]{:S(2)}) collective-permute-start(s32[1232,128]{1,0:T(8,128)S(1)} %get-tuple-element.14), channel_id=1, source_target_pairs={{8,12},{16,20},{24,28},{32,36},{40,44},{48,52},{56,60},{64,68},{72... | collective-permute-start | bytes 1892360 | tf_op jit(solution)/shard_map/ppermute | solution.py:354
  19.9 23.8 %collective-permute-start.4 = (s32[1232,128]{1,0:T(8,128)S(1)}, s32[1232,128]{1,0:T(8,128)S(1)}, u32[]{:S(2)}, u32[]{:S(2)}) collective-permute-start(s32[1232,128]{1,0:T(8,128)S(1)} %get-tuple-element.15), channel_id=1, source_target_pairs={{4,8},{12,16},{20,24},{28,32},{36,40},{44,48},{52,56},{60,64},{68,... | collective-permute-start | bytes 1892360 | tf_op jit(solution)/shard_map/ppermute | solution.py:354

commit v5 on v4

--- a/solution.py
+++ b/solution.py
@@ -108,13 +108,14 @@
 
 
 def sweep_kernel(
-    near_top, near, far, side, words, accept, table, final, means, edge0, edge1, side_planes, packed, spins, sems
+    near_top, corner_top, near, far, side, words, accept, table, final, means, edge0, edge1, side_planes, packed, spins, sems
 ):
     sub, lane, even = iotas()
     odd = jnp.logical_not(even)
 
     def from_near(row):
-        return near_top[pl.ds(row, 8), :] | near[pl.ds(row, 8), :]
+        first = corner_top[pl.ds(row - SIDE_AT, 8), :] if row >= SIDE_AT else near_top[pl.ds(row, 8), :]
+        return first | near[pl.ds(row, 8), :]
 
     def from_far(row):
         return far[pl.ds(row, 8), :]
@@ -295,9 +296,9 @@
             target = tiles.at[side, pl.ds(32 * n, 32), :]
             copies.append(pltpu.make_async_copy(ref.at[:, column], target, sem.at[len(copies)]))
             copies[-1].start()
-    for copy in copies:
-        copy.wait()
     for side, target, is_last in ((0, to_other, jnp.logical_not(cols_are_even())), (1, to_partner, cols_are_even())):
+        for copy in copies[3 * side : 3 * side + 3]:
+            copy.wait()
         skip = jnp.where(is_last, 16, 0)
         packed = [jnp.zeros((8, LANES), I32)] * 2
         for k in range(12):
@@ -311,7 +312,26 @@
 MESSAGE = SIDE_AT + 16
 
 
-def rows_kernel(lattice, draws, from_partner, from_other, side, near, far):
+def write_rows(lattice, draws, target, down):
+    below = (((2, 24), 30), ((1, 24), 23), ((1, 16), 15), ((0, 24), 8), ((0, 16), 0))
+    above = (((0, 0), 0), ((0, 8), 8), ((1, 0), 16), ((1, 8), 24), ((2, 0), 31))
+    for g in range(GROUPS):
+        for (n, row), at in below if down else above:
+            ref = lattice if n == 0 else draws.at[n - 1]
+            target[pl.ds(DEEP * g + at, 8), :] = ref[pl.ds(row, 8), pl.ds(g * LANES, LANES)]
+
+
+def top_kernel(lattice, draws, top):
+    @pl.when(rows_are_even())
+    def _():
+        write_rows(lattice, draws, top, True)
+
+    @pl.when(jnp.logical_not(rows_are_even()))
+    def _():
+        write_rows(lattice, draws, top, False)
+
+
+def rows_kernel(lattice, draws, from_partner, from_other, side, near, far, corner):
     lane = lax.broadcasted_iota(I32, (8, LANES), 1)
     partner_is_right = cols_are_even()
     low = (lane < LANES // 2) == partner_is_right
@@ -323,12 +343,7 @@
         side[pl.ds(8 * k, 8), :] = jnp.where(low, partner, other)
 
     def write(target, down):
-        below = (((2, 24), 30), ((1, 24), 23), ((1, 16), 15), ((0, 24), 8), ((0, 16), 0))
-        above = (((0, 0), 0), ((0, 8), 8), ((1, 0), 16), ((1, 8), 24), ((2, 0), 31))
-        for g in range(GROUPS):
-            for (n, row), at in below if down else above:
-                ref = lattice if n == 0 else draws.at[n - 1]
-                target[pl.ds(DEEP * g + at, 8), :] = ref[pl.ds(row, 8), pl.ds(g * LANES, LANES)]
+        write_rows(lattice, draws, target, down)
         start = 16 if down else 0
         dense = jnp.zeros((8, LANES), I32)
         for k, row in enumerate((start, start + 8, 32 + start, 40 + start, 88 if down else 64)):
@@ -346,6 +361,8 @@
     def _():
         write(far, True)
         write(near, False)
+
+    corner[...] = near[pl.ds(SIDE_AT, 16), :]
 
 
 def swap(x, axis, first, only=None):
@@ -381,15 +398,18 @@
     from_other = swap(to_other, "cols", 1)
     from_partner = swap(to_partner, "cols", 0)
 
-    side, to_near, to_far = call(
+    to_top = call(top_kernel, words(SIDE_AT + 8, LANES), 1_000_000, (lattice, draws))
+    near_top = swap(to_top, "rows", 0, slice(0, 1))
+    side, to_near, to_far, to_corner = call(
         rows_kernel,
-        (words(96, LANES), words(MESSAGE, LANES), words(MESSAGE, LANES)),
+        (words(96, LANES), words(MESSAGE, LANES), words(MESSAGE, LANES), words(16, LANES)),
         1_000_000,
         (lattice, draws, from_partner, from_other),
     )
-    near_top = swap(to_near, "rows", 0, slice(0, 1))
     far = swap(to_far, "rows", 1)
     near = swap(to_near, "rows", 0, slice(1, None))
+
+    corner_top = swap(to_corner, "rows", 0, slice(0, 1))
 
     accept, spins, table = call(
         own_kernel,
@@ -404,8 +424,8 @@
         sweep_kernel,
         (words(32, width), jax.ShapeDtypeStruct((1, 32), jnp.float32)),
         40_000_000,
-        (near_top, near, far, side, spins, accept, table),
-        in_specs=[vmem] * 7,
+        (near_top, corner_top, near, far, side, spins, accept, table),
+        in_specs=[vmem] * 8,
         out_specs=(pl.BlockSpec(memory_space=pltpu.HBM), vmem),
         scratch_shapes=[
             pltpu.VMEM((2, 2, 32, 8, LANES), I32),

time: 54.7 us -> 57.5 us (1.051)
  starting transfers between devices: 22.9 us -> 27.4 us
  waiting for transfers between devices: 16.5 us -> 14.1 us
    ppermute x5 -> x6, starting transfers between devices: 22.9 us -> 27.4 us  [swap(): return lax.ppermute(x, axis, pairs + [(j, i) for i, j in pairs])]
    ppermute x5 -> x6, waiting for transfers between devices: 16.5 us -> 14.1 us  [swap(): return lax.ppermute(x, axis, pairs + [(j, i) for i, j in pairs])]
    pallas_call x4 -> x5, Pallas kernels: 6.41 us -> 6.49 us  [call(): pl.pallas_call(kernel, out_shape=out_shape, compiler_params=pltpu.Compile...]
  transfers between devices with their start and end apart: 5 -> 6, of which waited for: 3 -> 2; matrix products, arithmetic and copies ran while one was open for 0% -> 0% of each run, Pallas kernels for 4% -> 4%
where the time goes in v5:
time: 57.5 us; the launch traced here: 57.2 us
  starting transfers between devices  27.4 us (48%)
  waiting for transfers between devices  14.1 us (25%)
  blocking collectives  8.47 us (15%)
  Pallas kernels  6.49 us (11%)
  between operations  0.75 us (1%)
    ppermute x6, starting transfers between devices, swap(): return lax.ppermute(x, axis, pairs + [(j, i) for i, j in pairs])  27.4 us
    ppermute x6, waiting for transfers between devices, swap(): return lax.ppermute(x, axis, pairs + [(j, i) for i, j in pairs])  14.1 us
    psum x1, blocking collectives, on_device(): return (final, lax.psum(means, 'cols').reshape(32))  8.47 us
    pallas_call x5, Pallas kernels, call(): pl.pallas_call(kernel, out_shape=out_shape, compiler_params=pltpu.Compile...  6.49 us
  transfers between devices with their start and end apart: 6, of which 2 were waited for; matrix products, arithmetic and copies ran while one was open for 0% of the time, Pallas kernels for 4%

profile of v5, /device:TPU:1, one launch (start us, length us, event | category | flops | bytes accessed | tf_op | source)
XLA Modules:
  0.0 57.2 jit_solution(15193050580895453431)
XLA Ops:
  0.6 0.0 copy-start.1
  0.6 0.0 copy-start
  0.6 1.1 %shard_map.51 = (s32[16,128]{1,0:T(8,128)S(1)}, s32[16,128]{1,0:T(8,128)S(1)}) custom-call(s32[32,4096]{1,0:T(8,128)} %lattice.7, s32[2,32,4096]{2,1,0:T(8,128)} %draws.7), custom_call_target="tpu_custom_call" | custom-call | flops 1000000 | bytes 2000000 | tf_op jit(solution)/shard_map/pallas_call | solution.py:379
  1.8 8.7 %collective-permute-start.1 = (s32[16,128]{1,0:T(8,128)S(1)}, s32[16,128]{1,0:T(8,128)S(1)}, u32[]{:S(2)}, u32[]{:S(2)}) collective-permute-start(s32[16,128]{1,0:T(8,128)S(1)} %get-tuple-element.13), channel_id=1, source_target_pairs={{0,1},{2,3},{1,0},{3,2},{4,5},{6,7},{5,4},{7,6},{8,9},{10,11},{9,8... | collective-permute-start | bytes 24584 | tf_op jit(solution)/shard_map/ppermute | solution.py:371
  10.5 1.9 %collective-permute-start.2 = (s32[16,128]{1,0:T(8,128)S(1)}, s32[16,128]{1,0:T(8,128)S(1)}, u32[]{:S(2)}, u32[]{:S(2)}) collective-permute-start(s32[16,128]{1,0:T(8,128)S(1)} %get-tuple-element.14), channel_id=1, source_target_pairs={{1,2},{3,0},{2,1},{0,3},{5,6},{7,4},{6,5},{4,7},{9,10},{11,8},{10,... | collective-permute-start | bytes 24584 | tf_op jit(solution)/shard_map/ppermute | solution.py:371
  12.4 0.0 collective-permute-done.1.from_partner
  12.5 4.5 %collective-permute-done.2.from_other = s32[16,128]{1,0:T(8,128)S(1)} collective-permute-done((s32[16,128]{1,0:T(8,128)S(1)}, s32[16,128]{1,0:T(8,128)S(1)}, u32[]{:S(2)}, u32[]{:S(2)}) %collective-permute-start.2) | collective-permute-done | bytes 8224 | tf_op jit(solution)/shard_map/ppermute | solution.py:371
  17.0 0.0 copy-done.1
  17.0 0.0 copy-done
  17.0 0.2 shard_map.52
  17.2 0.7 %collective-permute-start.4 = (s32[1232,128]{1,0:T(8,128)S(1)}, s32[1232,128]{1,0:T(8,128)S(1)}, u32[]{:S(2)}, u32[]{:S(2)}) collective-permute-start(s32[1232,128]{1,0:T(8,128)S(1)} %get-tuple-element.16), channel_id=1, source_target_pairs={{8,12},{16,20},{24,28},{32,36},{40,44},{48,52},{56,60},{64,68},{72... | collective-permute-start | bytes 1892360 | tf_op jit(solution)/shard_map/ppermute | solution.py:371
  17.9 10.7 %collective-permute-start.5 = (s32[1232,128]{1,0:T(8,128)S(1)}, s32[1232,128]{1,0:T(8,128)S(1)}, u32[]{:S(2)}, u32[]{:S(2)}) collective-permute-start(s32[1232,128]{1,0:T(8,128)S(1)} %get-tuple-element.17), channel_id=1, source_target_pairs={{4,8},{12,16},{20,24},{28,32},{36,40},{44,48},{52,56},{60,64},{68,... | collective-permute-start | bytes 1892360 | tf_op jit(solution)/shard_map/ppermute | solution.py:371
  28.7 0.1 shard_map.50
  28.7 0.0 copy-start.2
  28.7 1.9 %collective-permute-start = (s32[1224,128]{1,0:T(8,128)S(1)}, s32[1224,128]{1,0:T(8,128)S(1)}, u32[]{:S(2)}, u32[]{:S(2)}) collective-permute-start(s32[1224,128]{1,0:T(8,128)S(1)} %shard_map.50), channel_id=1, source_target_pairs={{0,4},{4,0},{1,5},{5,1},{2,6},{6,2},{3,7},{7,3}} | collective-permute-start | bytes 1880072 | tf_op jit(solution)/shard_map/ppermute | solution.py:371
  30.7 3.4 %collective-permute-start.3 = (s32[16,128]{1,0:T(8,128)S(1)}, s32[16,128]{1,0:T(8,128)S(1)}, u32[]{:S(2)}, u32[]{:S(2)}) collective-permute-start(s32[16,128]{1,0:T(8,128)S(1)} %get-tuple-element.15), channel_id=1, source_target_pairs={{0,4},{4,0},{1,5},{5,1},{2,6},{6,2},{3,7},{7,3}} | collective-permute-start | bytes 24584 | tf_op jit(solution)/shard_map/ppermute | solution.py:371
  34.0 0.0 copy-done.2
  34.0 2.3 %shard_map.53 = (s32[2,2,8,5,8,128]{5,4,3,2,1,0:T(8,128)S(1)}, s32[2,2,8,128]{3,2,1,0:T(8,128)S(1)}, s32[2,8,5,8,128]{4,3,2,1,0:T(8,128)S(1)}) custom-call(s32[5]{0:T(128)S(1)} %copy-done.2, s32[32,4096]{1,0:T(8,128)S(1)} %copy-done.1, s32[2,32,4096]{2,1,0:T(8,128)S(1)} %copy-done), custom_call_target="tpu_custom_call" | custom-call | flops 50000000 | bytes 2000000 | tf_op jit(solution)/shard_map/pallas_call | solution.py:379
  36.4 9.5 %collective-permute-done.3.corner_top = s32[16,128]{1,0:T(8,128)S(1)} collective-permute-done((s32[16,128]{1,0:T(8,128)S(1)}, s32[16,128]{1,0:T(8,128)S(1)}, u32[]{:S(2)}, u32[]{:S(2)}) %collective-permute-start.3) | collective-permute-done | bytes 8224 | tf_op jit(solution)/shard_map/ppermute | solution.py:371
  45.9 0.0 collective-permute-done.near_top
  45.9 0.0 collective-permute-done.4.near
  45.9 0.0 collective-permute-done.5.far
  45.9 2.8 %shard_map.54 = (s32[32,4096]{1,0:T(8,128)}, f32[1,32]{1,0:T(1,128)S(1)}) custom-call(s32[1224,128]{1,0:T(8,128)S(1)} %collective-permute-done.near_top, s32[16,128]{1,0:T(8,128)S(1)} %collective-permute-done.3.corner_top, s32[1232,128]{1,0:T(8,128)S(1)} %collective-permute-done.4.near, s32[1232,128]{1,0:T(8,128)S(1)} %collective-permute-done.5.far, ...), custom_call_target="tpu_custom_call" | custom-call | flops 40000000 | bytes 2000000 | tf_op jit(solution)/shard_map/pallas_call | solution.py:379
  48.7 8.5 %psum.7 = f32[32]{0:T(128)} all-reduce(f32[32]{0:T(128)S(1)} %bitcast.1), channel_id=1, replica_groups=mesh['rows'=128,'cols'=4] {'cols'}, use_global_device_ids=true, to_apply=%region_0.0 | all-reduce | flops 32 | bytes 256 | tf_op jit(solution)/shard_map/psum | solution.py:439
Async XLA Ops:
  0.6 16.4 %copy-start.1 = (s32[32,4096]{1,0:T(8,128)S(1)}, s32[32,4096]{1,0:T(8,128)}, u32[]{:S(2)}) copy-start(s32[32,4096]{1,0:T(8,128)} %lattice.7) | copy-start | bytes 1572868
  0.6 16.4 %copy-start = (s32[2,32,4096]{2,1,0:T(8,128)S(1)}, s32[2,32,4096]{2,1,0:T(8,128)}, u32[]{:S(2)}) copy-start(s32[2,32,4096]{2,1,0:T(8,128)} %draws.7) | copy-start | bytes 3145732
  1.8 10.7 %collective-permute-start.1 = (s32[16,128]{1,0:T(8,128)S(1)}, s32[16,128]{1,0:T(8,128)S(1)}, u32[]{:S(2)}, u32[]{:S(2)}) collective-permute-start(s32[16,128]{1,0:T(8,128)S(1)} %get-tuple-element.13), channel_id=1, source_target_pairs={{0,1},{2,3},{1,0},{3,2},{4,5},{6,7},{5,4},{7,6},{8,9},{10,11},{9,8... | collective-permute-start | bytes 24584 | tf_op jit(solution)/shard_map/ppermute | solution.py:371
  10.5 6.5 %collective-permute-start.2 = (s32[16,128]{1,0:T(8,128)S(1)}, s32[16,128]{1,0:T(8,128)S(1)}, u32[]{:S(2)}, u32[]{:S(2)}) collective-permute-start(s32[16,128]{1,0:T(8,128)S(1)} %get-tuple-element.14), channel_id=1, source_target_pairs={{1,2},{3,0},{2,1},{0,3},{5,6},{7,4},{6,5},{4,7},{9,10},{11,8},{10,... | collective-permute-start | bytes 24584 | tf_op jit(solution)/shard_map/ppermute | solution.py:371
  17.2 28.7 %collective-permute-start.4 = (s32[1232,128]{1,0:T(8,128)S(1)}, s32[1232,128]{1,0:T(8,128)S(1)}, u32[]{:S(2)}, u32[]{:S(2)}) collective-permute-start(s32[1232,128]{1,0:T(8,128)S(1)} %get-tuple-element.16), channel_id=1, source_target_pairs={{8,12},{16,20},{24,28},{32,36},{40,44},{48,52},{56,60},{64,68},{72... | collective-permute-start | bytes 1892360 | tf_op jit(solution)/shard_map/ppermute | solution.py:371
  17.9 28.0 %collective-permute-start.5 = (s32[1232,128]{1,0:T(8,128)S(1)}, s32[1232,128]{1,0:T(8,128)S(1)}, u32[]{:S(2)}, u32[]{:S(2)}) collective-permute-start(s32[1232,128]{1,0:T(8,128)S(1)} %get-tuple-element.17), channel_id=1, source_target_pairs={{4,8},{12,16},{20,24},{28,32},{36,40},{44,48},{52,56},{60,64},{68,... | collective-permute-start | bytes 1892360 | tf_op jit(solution)/shard_map/ppermute | solution.py:371
  28.7 5.3 %copy-start.2 = (s32[5]{0:T(128)S(1)}, s32[5]{0:T(128)}, u32[]{:S(2)}) copy-start(s32[5]{0:T(128)} %thresholds.1) | copy-start | bytes 64
  28.7 17.2 %collective-permute-start = (s32[1224,128]{1,0:T(8,128)S(1)}, s32[1224,128]{1,0:T(8,128)S(1)}, u32[]{:S(2)}, u32[]{:S(2)}) collective-permute-start(s32[1224,128]{1,0:T(8,128)S(1)} %shard_map.50), channel_id=1, source_target_pairs={{0,4},{4,0},{1,5},{5,1},{2,6},{6,2},{3,7},{7,3}} | collective-permute-start | bytes 1880072 | tf_op jit(solution)/shard_map/ppermute | solution.py:371
  30.7 15.2 %collective-permute-start.3 = (s32[16,128]{1,0:T(8,128)S(1)}, s32[16,128]{1,0:T(8,128)S(1)}, u32[]{:S(2)}, u32[]{:S(2)}) collective-permute-start(s32[16,128]{1,0:T(8,128)S(1)} %get-tuple-element.15), channel_id=1, source_target_pairs={{0,4},{4,0},{1,5},{5,1},{2,6},{6,2},{3,7},{7,3}} | collective-permute-start | bytes 24584 | tf_op jit(solution)/shard_map/ppermute | solution.py:371

commit v6 on v5

--- a/solution.py
+++ b/solution.py
@@ -321,17 +321,21 @@
             target[pl.ds(DEEP * g + at, 8), :] = ref[pl.ds(row, 8), pl.ds(g * LANES, LANES)]
 
 
-def top_kernel(lattice, draws, top):
+def main_kernel(lattice, draws, top, near, far):
     @pl.when(rows_are_even())
     def _():
         write_rows(lattice, draws, top, True)
+        write_rows(lattice, draws, near, True)
+        write_rows(lattice, draws, far, False)
 
     @pl.when(jnp.logical_not(rows_are_even()))
     def _():
         write_rows(lattice, draws, top, False)
-
-
-def rows_kernel(lattice, draws, from_partner, from_other, side, near, far, corner):
+        write_rows(lattice, draws, near, False)
+        write_rows(lattice, draws, far, True)
+
+
+def rows_kernel(from_partner, from_other, near_main, far_main, side, near, far, corner):
     lane = lax.broadcasted_iota(I32, (8, LANES), 1)
     partner_is_right = cols_are_even()
     low = (lane < LANES // 2) == partner_is_right
@@ -343,7 +347,6 @@
         side[pl.ds(8 * k, 8), :] = jnp.where(low, partner, other)
 
     def write(target, down):
-        write_rows(lattice, draws, target, down)
         start = 16 if down else 0
         dense = jnp.zeros((8, LANES), I32)
         for k, row in enumerate((start, start + 8, 32 + start, 40 + start, 88 if down else 64)):
@@ -398,13 +401,15 @@
     from_other = swap(to_other, "cols", 1)
     from_partner = swap(to_partner, "cols", 0)
 
-    to_top = call(top_kernel, words(SIDE_AT + 8, LANES), 1_000_000, (lattice, draws))
+    message = words(MESSAGE, LANES)
+    to_top, near_main, far_main = call(main_kernel, (words(SIDE_AT + 8, LANES), message, message), 1_000_000, (lattice, draws))
     near_top = swap(to_top, "rows", 0, slice(0, 1))
     side, to_near, to_far, to_corner = call(
         rows_kernel,
-        (words(96, LANES), words(MESSAGE, LANES), words(MESSAGE, LANES), words(16, LANES)),
+        (words(96, LANES), message, message, words(16, LANES)),
         1_000_000,
-        (lattice, draws, from_partner, from_other),
+        (from_partner, from_other, near_main, far_main),
+        input_output_aliases={2: 1, 3: 2},
     )
     far = swap(to_far, "rows", 1)
     near = swap(to_near, "rows", 0, slice(1, None))

time: 57.5 us -> 57.5 us (level)
  no operation moved by 1% of the time
where the time goes in v6:
time: 57.5 us; the launch traced here: 57.2 us
  starting transfers between devices  27.4 us (48%)
  waiting for transfers between devices  13.8 us (24%)
  blocking collectives  8.47 us (15%)
  Pallas kernels  6.71 us (12%)
  between operations  0.77 us (1%)
    ppermute x6, starting transfers between devices, swap(): return lax.ppermute(x, axis, pairs + [(j, i) for i, j in pairs])  27.4 us
    ppermute x6, waiting for transfers between devices, swap(): return lax.ppermute(x, axis, pairs + [(j, i) for i, j in pairs])  13.8 us
    psum x1, blocking collectives, on_device(): return (final, lax.psum(means, 'cols').reshape(32))  8.47 us
    pallas_call x5, Pallas kernels, call(): pl.pallas_call(kernel, out_shape=out_shape, compiler_params=pltpu.Compile...  6.71 us
  transfers between devices with their start and end apart: 6, of which 2 were waited for; matrix products, arithmetic and copies ran while one was open for 0% of the time, Pallas kernels for 4%

profile of v6, /device:TPU:1, one launch (start us, length us, event | category | flops | bytes accessed | tf_op | source)
XLA Modules:
  0.0 57.2 jit_solution(2200563761864231454)
XLA Ops:
  0.6 0.0 copy-start.1
  0.6 0.0 copy-start
  0.6 1.1 %shard_map.51 = (s32[16,128]{1,0:T(8,128)S(1)}, s32[16,128]{1,0:T(8,128)S(1)}) custom-call(s32[32,4096]{1,0:T(8,128)} %lattice.5, s32[2,32,4096]{2,1,0:T(8,128)} %draws.5), custom_call_target="tpu_custom_call" | custom-call | flops 1000000 | bytes 2000000 | tf_op jit(solution)/shard_map/pallas_call | solution.py:382
  1.8 8.7 %collective-permute-start.1 = (s32[16,128]{1,0:T(8,128)S(1)}, s32[16,128]{1,0:T(8,128)S(1)}, u32[]{:S(2)}, u32[]{:S(2)}) collective-permute-start(s32[16,128]{1,0:T(8,128)S(1)} %get-tuple-element.17), channel_id=1, source_target_pairs={{0,1},{2,3},{1,0},{3,2},{4,5},{6,7},{5,4},{7,6},{8,9},{10,11},{9,8... | collective-permute-start | bytes 24584 | tf_op jit(solution)/shard_map/ppermute | solution.py:374
  10.5 1.9 %collective-permute-start.2 = (s32[16,128]{1,0:T(8,128)S(1)}, s32[16,128]{1,0:T(8,128)S(1)}, u32[]{:S(2)}, u32[]{:S(2)}) collective-permute-start(s32[16,128]{1,0:T(8,128)S(1)} %get-tuple-element.18), channel_id=1, source_target_pairs={{1,2},{3,0},{2,1},{0,3},{5,6},{7,4},{6,5},{4,7},{9,10},{11,8},{10,... | collective-permute-start | bytes 24584 | tf_op jit(solution)/shard_map/ppermute | solution.py:374
  12.4 0.0 copy-done.1
  12.5 0.0 copy-done
  12.5 0.1 shard_map.50
  12.6 0.0 collective-permute-done.1.from_partner
  12.6 4.4 %collective-permute-done.2.from_other = s32[16,128]{1,0:T(8,128)S(1)} collective-permute-done((s32[16,128]{1,0:T(8,128)S(1)}, s32[16,128]{1,0:T(8,128)S(1)}, u32[]{:S(2)}, u32[]{:S(2)}) %collective-permute-start.2) | collective-permute-done | bytes 8224 | tf_op jit(solution)/shard_map/ppermute | solution.py:374
  17.0 0.2 shard_map.52
  17.2 0.7 %collective-permute-start.4 = (s32[1232,128]{1,0:T(8,128)S(1)}, s32[1232,128]{1,0:T(8,128)S(1)}, u32[]{:S(2)}, u32[]{:S(2)}) collective-permute-start(s32[1232,128]{1,0:T(8,128)S(1)} %get-tuple-element.22), channel_id=1, source_target_pairs={{8,12},{16,20},{24,28},{32,36},{40,44},{48,52},{56,60},{64,68},{72... | collective-permute-start | bytes 1892360 | tf_op jit(solution)/shard_map/ppermute | solution.py:374
  17.9 10.7 %collective-permute-start.5 = (s32[1232,128]{1,0:T(8,128)S(1)}, s32[1232,128]{1,0:T(8,128)S(1)}, u32[]{:S(2)}, u32[]{:S(2)}) collective-permute-start(s32[1232,128]{1,0:T(8,128)S(1)} %get-tuple-element.23), channel_id=1, source_target_pairs={{4,8},{12,16},{20,24},{28,32},{36,40},{44,48},{52,56},{60,64},{68,... | collective-permute-start | bytes 1892360 | tf_op jit(solution)/shard_map/ppermute | solution.py:374
  28.6 0.0 copy-start.2
  28.6 1.9 %collective-permute-start = (s32[1224,128]{1,0:T(8,128)S(1)}, s32[1224,128]{1,0:T(8,128)S(1)}, u32[]{:S(2)}, u32[]{:S(2)}) collective-permute-start(s32[1224,128]{1,0:T(8,128)S(1)} %get-tuple-element.16), channel_id=1, source_target_pairs={{0,4},{4,0},{1,5},{5,1},{2,6},{6,2},{3,7},{7,3}} | collective-permute-start | bytes 1880072 | tf_op jit(solution)/shard_map/ppermute | solution.py:374
  30.6 3.4 %collective-permute-start.3 = (s32[16,128]{1,0:T(8,128)S(1)}, s32[16,128]{1,0:T(8,128)S(1)}, u32[]{:S(2)}, u32[]{:S(2)}) collective-permute-start(s32[16,128]{1,0:T(8,128)S(1)} %get-tuple-element.21), channel_id=1, source_target_pairs={{0,4},{4,0},{1,5},{5,1},{2,6},{6,2},{3,7},{7,3}} | collective-permute-start | bytes 24584 | tf_op jit(solution)/shard_map/ppermute | solution.py:374
  33.9 0.0 copy-done.2
  34.0 2.4 %shard_map.53 = (s32[2,2,8,5,8,128]{5,4,3,2,1,0:T(8,128)S(1)}, s32[2,2,8,128]{3,2,1,0:T(8,128)S(1)}, s32[2,8,5,8,128]{4,3,2,1,0:T(8,128)S(1)}) custom-call(s32[5]{0:T(128)S(1)} %copy-done.2, s32[32,4096]{1,0:T(8,128)S(1)} %copy-done.1, s32[2,32,4096]{2,1,0:T(8,128)S(1)} %copy-done), custom_call_target="tpu_custom_call" | custom-call | flops 50000000 | bytes 2000000 | tf_op jit(solution)/shard_map/pallas_call | solution.py:382
  36.3 9.5 %collective-permute-done.3.corner_top = s32[16,128]{1,0:T(8,128)S(1)} collective-permute-done((s32[16,128]{1,0:T(8,128)S(1)}, s32[16,128]{1,0:T(8,128)S(1)}, u32[]{:S(2)}, u32[]{:S(2)}) %collective-permute-start.3) | collective-permute-done | bytes 8224 | tf_op jit(solution)/shard_map/ppermute | solution.py:374
  45.8 0.0 collective-permute-done.near_top
  45.8 0.0 collective-permute-done.4.near
  45.8 0.0 collective-permute-done.5.far
  45.8 2.9 %shard_map.54 = (s32[32,4096]{1,0:T(8,128)}, f32[1,32]{1,0:T(1,128)S(1)}) custom-call(s32[1224,128]{1,0:T(8,128)S(1)} %collective-permute-done.near_top, s32[16,128]{1,0:T(8,128)S(1)} %collective-permute-done.3.corner_top, s32[1232,128]{1,0:T(8,128)S(1)} %collective-permute-done.4.near, s32[1232,128]{1,0:T(8,128)S(1)} %collective-permute-done.5.far, ...), custom_call_target="tpu_custom_call" | custom-call | flops 40000000 | bytes 2000000 | tf_op jit(solution)/shard_map/pallas_call | solution.py:382
  48.7 8.5 %psum.7 = f32[32]{0:T(128)} all-reduce(f32[32]{0:T(128)S(1)} %bitcast.1), channel_id=1, replica_groups=mesh['rows'=128,'cols'=4] {'cols'}, use_global_device_ids=true, to_apply=%region_0.0 | all-reduce | flops 32 | bytes 256 | tf_op jit(solution)/shard_map/psum | solution.py:444
Async XLA Ops:
  0.6 11.8 %copy-start.1 = (s32[32,4096]{1,0:T(8,128)S(1)}, s32[32,4096]{1,0:T(8,128)}, u32[]{:S(2)}) copy-start(s32[32,4096]{1,0:T(8,128)} %lattice.5) | copy-start | bytes 1572868
  0.6 11.8 %copy-start = (s32[2,32,4096]{2,1,0:T(8,128)S(1)}, s32[2,32,4096]{2,1,0:T(8,128)}, u32[]{:S(2)}) copy-start(s32[2,32,4096]{2,1,0:T(8,128)} %draws.5) | copy-start | bytes 3145732
  1.8 10.9 %collective-permute-start.1 = (s32[16,128]{1,0:T(8,128)S(1)}, s32[16,128]{1,0:T(8,128)S(1)}, u32[]{:S(2)}, u32[]{:S(2)}) collective-permute-start(s32[16,128]{1,0:T(8,128)S(1)} %get-tuple-element.17), channel_id=1, source_target_pairs={{0,1},{2,3},{1,0},{3,2},{4,5},{6,7},{5,4},{7,6},{8,9},{10,11},{9,8... | collective-permute-start | bytes 24584 | tf_op jit(solution)/shard_map/ppermute | solution.py:374
  10.5 6.5 %collective-permute-start.2 = (s32[16,128]{1,0:T(8,128)S(1)}, s32[16,128]{1,0:T(8,128)S(1)}, u32[]{:S(2)}, u32[]{:S(2)}) collective-permute-start(s32[16,128]{1,0:T(8,128)S(1)} %get-tuple-element.18), channel_id=1, source_target_pairs={{1,2},{3,0},{2,1},{0,3},{5,6},{7,4},{6,5},{4,7},{9,10},{11,8},{10,... | collective-permute-start | bytes 24584 | tf_op jit(solution)/shard_map/ppermute | solution.py:374
  17.2 28.6 %collective-permute-start.4 = (s32[1232,128]{1,0:T(8,128)S(1)}, s32[1232,128]{1,0:T(8,128)S(1)}, u32[]{:S(2)}, u32[]{:S(2)}) collective-permute-start(s32[1232,128]{1,0:T(8,128)S(1)} %get-tuple-element.22), channel_id=1, source_target_pairs={{8,12},{16,20},{24,28},{32,36},{40,44},{48,52},{56,60},{64,68},{72... | collective-permute-start | bytes 1892360 | tf_op jit(solution)/shard_map/ppermute | solution.py:374
  17.9 27.9 %collective-permute-start.5 = (s32[1232,128]{1,0:T(8,128)S(1)}, s32[1232,128]{1,0:T(8,128)S(1)}, u32[]{:S(2)}, u32[]{:S(2)}) collective-permute-start(s32[1232,128]{1,0:T(8,128)S(1)} %get-tuple-element.23), channel_id=1, source_target_pairs={{4,8},{12,16},{20,24},{28,32},{36,40},{44,48},{52,56},{60,64},{68,... | collective-permute-start | bytes 1892360 | tf_op jit(solution)/shard_map/ppermute | solution.py:374
  28.6 5.3 %copy-start.2 = (s32[5]{0:T(128)S(1)}, s32[5]{0:T(128)}, u32[]{:S(2)}) copy-start(s32[5]{0:T(128)} %thresholds.1) | copy-start | bytes 64
  28.6 17.2 %collective-permute-start = (s32[1224,128]{1,0:T(8,128)S(1)}, s32[1224,128]{1,0:T(8,128)S(1)}, u32[]{:S(2)}, u32[]{:S(2)}) collective-permute-start(s32[1224,128]{1,0:T(8,128)S(1)} %get-tuple-element.16), channel_id=1, source_target_pairs={{0,4},{4,0},{1,5},{5,1},{2,6},{6,2},{3,7},{7,3}} | collective-permute-start | bytes 1880072 | tf_op jit(solution)/shard_map/ppermute | solution.py:374
  30.6 15.2 %collective-permute-start.3 = (s32[16,128]{1,0:T(8,128)S(1)}, s32[16,128]{1,0:T(8,128)S(1)}, u32[]{:S(2)}, u32[]{:S(2)}) collective-permute-start(s32[16,128]{1,0:T(8,128)S(1)} %get-tuple-element.21), channel_id=1, source_target_pairs={{0,4},{4,0},{1,5},{5,1},{2,6},{6,2},{3,7},{7,3}} | collective-permute-start | bytes 24584 | tf_op jit(solution)/shard_map/ppermute | solution.py:374
